TPU v7x, 32 devices: a whole 2x2x4 slice. The times are simulated.
32 devices in a mesh: row: 4 (over z), col: 2 (over x), dp: 4 (over y, core).
Axes of the slice: x: 2, y: 2, z: 4, core: 2. Of those that a mesh axis runs over, the one named last changes fastest.
Arguments:
- tokens: bfloat16 [1536, 6144], P('dp', 'row'), parts along dimension 0, may hold values from -120 to 120
- norm_gain: float32 [6144], P('row'), may hold values from 0.25 to 1.75
- qkv_weight: bfloat16 [6144, 3, 3072], P('row', None, 'col'), may hold values from -2.5 to 2.5
- out_weight: bfloat16 [3072, 6144], P('col', 'row'), may hold values from -0.109375 to 0.109375
Outputs:
- projected: bfloat16 [1536, 6144], P('dp', 'row'), parts along dimension 0
There are 4 independent parts, one for each index of `dp`. A program takes and returns all parts, laid end to end along the dimension named above; an argument that names none is the same for every part. Nothing has to cross between parts.
All inputs are finite; a program needn't handle non-finite values.
Results may differ from a plain program's by a relative error of at most 0.025.
Values may be sent and summed in bfloat16 or wider, within the bound.
A program may use at most 64 MiB of HBM per device.

v0:
```python
import functools
import math

import jax
import jax.numpy as jnp
from jax import lax
from jax.experimental import pallas as pl
from jax.experimental.pallas import tpu as pltpu
from jax.sharding import PartitionSpec as P

K = 128


EPSILON = 1e-05


def attend(queries, key_rows, value_rows):
    query_total = queries.shape[0]
    head_count = queries.shape[1] // K
    scaling = 1.0 / math.sqrt(K)
    split_keys = key_rows.reshape(key_rows.shape[0], head_count, K)
    split_values = value_rows.reshape(value_rows.shape[0], head_count, K)
    split_queries = queries.reshape(query_total, head_count, K)
    scores = (
        jnp.einsum("qhd,khd->hqk", split_queries, split_keys, preferred_element_type=jnp.float32)
        * scaling
    )
    largest = jnp.max(scores, axis=2, keepdims=True)
    exponent = jnp.exp(scores - largest)
    softmax_weights = (exponent / jnp.sum(exponent, axis=2, keepdims=True)).astype(jnp.bfloat16)
    mixed = jnp.einsum(
        "hqk,khd->qhd", softmax_weights, split_values, preferred_element_type=jnp.float32
    )
    result = mixed.astype(jnp.bfloat16)
    return result.reshape(query_total, head_count * K)


def shards(tokens, norm_gain, qkv_weight, out_weight):
    row_count, block_width = tokens.shape
    full_width = block_width * lax.axis_size("row")
    values = tokens.astype(jnp.float32)
    totals, squares = lax.psum(
        (jnp.sum(values, axis=1, keepdims=True), jnp.sum(values * values, axis=1, keepdims=True)),
        "row",
    )
    average = totals / full_width
    variance = squares / full_width - average * average
    centered = values - average
    normed = (centered * lax.rsqrt(variance + EPSILON) * norm_gain).astype(jnp.bfloat16)
    head_columns = qkv_weight.shape[2]
    partial_value = jnp.dot(
        normed,
        qkv_weight.reshape(block_width, 3 * head_columns),
        preferred_element_type=jnp.float32,
    )
    summed = lax.psum(partial_value.astype(jnp.bfloat16), "row").reshape(row_count, 3, head_columns)
    attended = attend(summed[:, 0], summed[:, 1], summed[:, 2])
    partial_out = jnp.dot(attended, out_weight, preferred_element_type=jnp.float32)
    return lax.psum(partial_out.astype(jnp.bfloat16), "col")


MESH = pl.DeviceIdType.MESH
WIDE = 2 * K
SKEW = 1
ROWS = 32
PIECE = 128
PARTS = 2


def sublayer_kernel(
    rows_n, cols_n, tok_hbm, gain_ref, w_hbm, wo_hbm, out_ref,
    tok, wide_w, stat_col, stats, normed, arrived, summed, attended, late_w,
    tok_sem, w_sem, late_sem, st_send, st_recv, rs_send, rs_recv, at_send, at_recv,
    lw_send, lw_recv, fw_send, fw_recv, la_send, la_recv,
):
    z = lax.axis_index("row")
    col = lax.axis_index("col")
    tokens_n, block = tok.shape
    half = w_hbm.shape[2] // 2
    pairs = half // WIDE
    chunks = 3 * pairs
    tiles = block // WIDE
    pieces = tokens_n // PIECE
    part_rows = tokens_n // PARTS
    partner = {"col": 1 - col}
    scaling = 1.0 / math.sqrt(K)

    def weight_copy(d, c):
        pair, kind = c // 3, c % 3
        first = pl.multiple_of(d * half + pair * WIDE, WIDE)
        return pltpu.make_async_copy(
            w_hbm.at[kind, :, pl.ds(first, WIDE)], wide_w.at[d, c], w_sem.at[d, c]
        )

    tok_copy = pltpu.make_async_copy(tok_hbm, tok, tok_sem)
    tok_copy.start()

    @pl.loop(0, chunks)
    def _(c):
        weight_copy(0, c).start()
        weight_copy(1, c).start()

    dp = lax.axis_index("dp")
    side = dp % 2
    sibling = {"dp": dp + 1 - 2 * side}
    split = WIDE // 2

    def own_copy(d, p):
        rows = pl.ds(d * half + p * WIDE, WIDE)
        return pltpu.make_async_copy(wo_hbm.at[rows], late_w.at[col, d, p], late_sem.at[d, p])

    def share_copy(d, p, owner):
        first = pl.multiple_of(d * half + p * WIDE + side * split, split)
        at = pl.ds(pl.multiple_of(side * split, split), split)
        return pltpu.make_async_remote_copy(
            src_ref=wo_hbm.at[pl.ds(first, split)], dst_ref=late_w.at[owner, d, p, at],
            send_sem=lw_send.at[d, p], recv_sem=lw_recv.at[d, p], device_id=partner,
            device_id_type=MESH,
        )

    def hand_copy(d, p, which):
        piece = late_w.at[1 - col, d, p, pl.ds(pl.multiple_of(which * split, split), split)]
        return pltpu.make_async_remote_copy(
            src_ref=piece, dst_ref=piece, send_sem=fw_send.at[d, p],
            recv_sem=fw_recv.at[d, p], device_id=sibling, device_id_type=MESH,
        )

    blocks = [(d, p) for p in range(pairs) for d in range(2)]
    for d, p in blocks:
        own_copy(d, p).start()

    barrier = pltpu.get_barrier_semaphore()
    for o in range(1, rows_n):
        pl.semaphore_signal(
            barrier, inc=1, device_id={"row": lax.rem(z + o, rows_n)}, device_id_type=MESH
        )
    pl.semaphore_signal(barrier, inc=1, device_id=partner, device_id_type=MESH)
    pl.semaphore_signal(barrier, inc=1, device_id=sibling, device_id_type=MESH)

    tok_copy.wait()

    @pl.loop(0, tokens_n // ROWS)
    def _(i):
        at = pl.ds(pl.multiple_of(i * ROWS, ROWS), ROWS)
        x = tok[at, :].astype(jnp.float32)
        mean = jnp.sum(x, axis=1, keepdims=True) * (1.0 / block)
        away = x - mean
        square = jnp.sum(away * away, axis=1, keepdims=True)
        stat_col[0, at, :] = jnp.broadcast_to(mean, (ROWS, 128))
        stat_col[1, at, :] = jnp.broadcast_to(square, (ROWS, 128))

    stats[z, 0] = stat_col[0].T[0:8]
    stats[z, 1] = stat_col[1].T[0:8]
    pl.semaphore_wait(barrier, rows_n + 1)

    def stat_copy(o):
        return pltpu.make_async_remote_copy(
            src_ref=stats.at[z], dst_ref=stats.at[z], send_sem=st_send.at[o],
            recv_sem=st_recv.at[z], device_id={"row": lax.rem(z + o, rows_n)},
            device_id_type=MESH,
        )

    def stat_arrival(o):
        source = lax.rem(z + o, rows_n)
        return pltpu.make_async_remote_copy(
            src_ref=stats.at[source], dst_ref=stats.at[source], send_sem=st_send.at[o],
            recv_sem=st_recv.at[source], device_id={"row": source}, device_id_type=MESH,
        )

    for o in range(1, rows_n):
        stat_copy(o).start()
    for d, p in blocks:
        share_copy(d, p, col).start()
    for o in range(1, rows_n):
        stat_arrival(o).wait_recv()
    mean = sum(stats[i, 0] for i in range(rows_n)) * (1.0 / rows_n)
    spread = sum(
        stats[i, 1] * (1.0 / block) + (stats[i, 0] - mean) * (stats[i, 0] - mean)
        for i in range(rows_n)
    ) * (1.0 / rows_n)
    scale = lax.rsqrt(spread + EPSILON)
    stat_col[0] = jnp.broadcast_to(mean[0:1], (128, tokens_n)).T
    stat_col[1] = jnp.broadcast_to(scale[0:1], (128, tokens_n)).T

    @pl.loop(0, tokens_n // ROWS)
    def _(i):
        at = pl.ds(pl.multiple_of(i * ROWS, ROWS), ROWS)
        x = tok[at, :].astype(jnp.float32)
        away = (x - stat_col[0, at, 0:1]) * stat_col[1, at, 0:1]
        normed[at, :] = (away * gain_ref[...]).astype(jnp.bfloat16)

    def place(d):
        return z if d == 1 else rows_n - 1 - z

    def onward(d):
        return {"row": jnp.clip(z + 1 if d == 1 else z - 1, 0, rows_n - 1)}

    def back(d):
        return {"row": jnp.clip(z - 1 if d == 1 else z + 1, 0, rows_n - 1)}

    def sum_copy(d, c, i):
        at = pl.ds(i * part_rows, part_rows)
        return pltpu.make_async_remote_copy(
            src_ref=summed.at[d, c, at], dst_ref=arrived.at[d, c, at],
            send_sem=rs_send.at[d, c, i], recv_sem=rs_recv.at[d, c, i],
            device_id=onward(d), device_id_type=MESH,
        )

    def attended_copy(d, p, i):
        piece = attended.at[col, d, p, pl.ds(i * PIECE, PIECE)]
        return pltpu.make_async_remote_copy(
            src_ref=piece, dst_ref=piece, send_sem=at_send.at[d, p, i],
            recv_sem=at_recv.at[d, p, i], device_id=back(d), device_id_type=MESH,
        )

    def cross_copy(d, p, i, owner):
        piece = attended.at[owner, d, p, pl.ds(i * PIECE, PIECE)]
        return pltpu.make_async_remote_copy(
            src_ref=piece, dst_ref=piece, send_sem=la_send.at[d, p, i],
            recv_sem=la_recv.at[d, p, i], device_id=partner, device_id_type=MESH,
        )

    def attend_piece(d, p, i):
        rows = pl.ds(i * PIECE, PIECE)
        for h in range(2):
            at = slice(h * K, (h + 1) * K)
            q = summed[d, 3 * p, rows, at]
            k = summed[d, 3 * p + 1, :, at]
            v = summed[d, 3 * p + 2, :, at]
            scores = lax.dot_general(
                q, k, (((1,), (1,)), ((), ())), preferred_element_type=jnp.float32
            ) * scaling
            exponent = jnp.exp(scores - jnp.max(scores, axis=1, keepdims=True))
            weights = exponent / jnp.sum(exponent, axis=1, keepdims=True)
            attended[col, d, p, rows, at] = jnp.dot(
                weights.astype(jnp.bfloat16), v, preferred_element_type=jnp.float32
            ).astype(jnp.bfloat16)

    last_place = rows_n - 1
    slots = chunks + 2 * SKEW * last_place
    hand_slots = [min(4 + 2 * b, slots - 1) for b in range(len(blocks))]

    @pl.loop(0, slots)
    def _(t):
        for d in range(2):
            pos = place(d)
            c = t - SKEW * pos

            @pl.when((c >= 0) & (c < chunks))
            def _():
                weight_copy(d, c).wait()
                part = jnp.dot(normed[...], wide_w[d, c], preferred_element_type=jnp.float32)

                for i in range(PARTS):
                    lo = i * part_rows
                    at = pl.ds(lo, part_rows)
                    share = part[lo:lo + part_rows]

                    @pl.when(pos == 0)
                    def _():
                        summed[d, c, at] = share.astype(jnp.bfloat16)

                    @pl.when(pos > 0)
                    def _():
                        sum_copy(d, c, i).wait_recv()
                        total = share + arrived[d, c, at].astype(jnp.float32)
                        summed[d, c, at] = total.astype(jnp.bfloat16)

                    @pl.when(pos < last_place)
                    def _():
                        sum_copy(d, c, i).start()

        for d in range(2):
            pos = place(d)
            e = t - SKEW * last_place - SKEW * (last_place - pos)
            p = e // 3

            @pl.when((e >= 0) & (e < chunks) & (e % 3 == 2))
            def _():
                for i in range(pieces):
                    @pl.when(pos == last_place)
                    def _():
                        attend_piece(d, p, i)

                    @pl.when(pos < last_place)
                    def _():
                        attended_copy(d, p, i).wait_recv()

                    @pl.when(pos > 0)
                    def _():
                        attended_copy(d, p, i).start()

                    cross_copy(d, p, i, col).start()

        for (d, p), slot in zip(blocks, hand_slots):
            @pl.when(t == slot)
            def _():
                share_copy(d, p, 1 - col).wait_recv()
                hand_copy(d, p, side).start()

    for d, p in blocks:
        own_copy(d, p).wait()
        hand_copy(d, p, 1 - side).wait_recv()
        for i in range(pieces):
            cross_copy(d, p, i, 1 - col).wait_recv()

    @pl.loop(0, tiles)
    def _(j):
        at = pl.ds(pl.multiple_of(j * WIDE, WIDE), WIDE)
        total = jnp.zeros((tokens_n, WIDE), jnp.float32)
        for owner in range(2):
            for d, p in blocks:
                total = total + jnp.dot(
                    attended[owner, d, p], late_w[owner, d, p, :, at],
                    preferred_element_type=jnp.float32,
                )
        out_ref[:, at] = total.astype(jnp.bfloat16)

    for o in range(1, rows_n):
        stat_copy(o).wait_send()
    for d in range(2):
        pos = place(d)

        @pl.when(pos < last_place)
        def _():
            @pl.loop(0, chunks)
            def _(c):
                for i in range(PARTS):
                    sum_copy(d, c, i).wait_send()

        @pl.when(pos > 0)
        def _():
            @pl.loop(0, pairs)
            def _(p):
                for i in range(pieces):
                    attended_copy(d, p, i).wait_send()

    for d, p in blocks:
        share_copy(d, p, col).wait_send()
        hand_copy(d, p, side).wait_send()
        for i in range(pieces):
            cross_copy(d, p, i, col).wait_send()


def fused_shards(rows_n, cols_n, tokens, norm_gain, qkv_weight, out_weight):
    tokens_n, block = tokens.shape
    head_columns = qkv_weight.shape[2]
    pairs = head_columns // (2 * WIDE)
    chunks = 3 * pairs
    pieces = tokens_n // PIECE
    any_space = pl.BlockSpec(memory_space=pl.ANY)
    vmem = pl.BlockSpec(memory_space=pltpu.VMEM)
    dma = pltpu.SemaphoreType.DMA
    bf16, f32 = jnp.bfloat16, jnp.float32
    return pl.pallas_call(
        functools.partial(sublayer_kernel, rows_n, cols_n),
        out_shape=jax.ShapeDtypeStruct((tokens_n, block), bf16),
        in_specs=[any_space, vmem, any_space, any_space],
        out_specs=vmem,
        scratch_shapes=[
            pltpu.VMEM((tokens_n, block), bf16),
            pltpu.VMEM((2, chunks, block, WIDE), bf16),
            pltpu.VMEM((2, tokens_n, 128), f32),
            pltpu.VMEM((rows_n, 2, 8, tokens_n), f32),
            pltpu.VMEM((tokens_n, block), bf16),
            pltpu.VMEM((2, chunks, tokens_n, WIDE), bf16),
            pltpu.VMEM((2, chunks, tokens_n, WIDE), bf16),
            pltpu.VMEM((2, 2, pairs, tokens_n, WIDE), bf16),
            pltpu.VMEM((2, 2, pairs, WIDE, block), bf16),
            dma, dma((2, chunks)), dma((2, pairs)),
            dma((rows_n,)), dma((rows_n,)),
            dma((2, chunks, PARTS)), dma((2, chunks, PARTS)),
            dma((2, pairs, pieces)), dma((2, pairs, pieces)),
            dma((2, pairs)), dma((2, pairs)), dma((2, pairs)), dma((2, pairs)),
            dma((2, pairs, pieces)), dma((2, pairs, pieces)),
        ],
        compiler_params=pltpu.CompilerParams(
            collective_id=0, has_side_effects=True, vmem_limit_bytes=60 * 1024 * 1024
        ),
    )(tokens, norm_gain.reshape(1, block), jnp.transpose(qkv_weight, (1, 0, 2)), out_weight)


def solution(mesh):
    in_specs = (P("dp", "row"), P("row"), P("row", None, "col"), P("col", "row"))
    out_specs = P("dp", "row")
    rows_n, cols_n = mesh.shape["row"], mesh.shape["col"]

    def body(tokens, norm_gain, qkv_weight, out_weight):
        tokens_n, block = tokens.shape
        fits = (
            cols_n == 2 and mesh.shape["dp"] % 2 == 0 and rows_n >= 2 and qkv_weight.shape[2] % (2 * WIDE) == 0
            and qkv_weight.shape[2] >= 4 * WIDE
            and block % WIDE == 0 and tokens_n % 128 == 0
        )
        if fits:
            return fused_shards(rows_n, cols_n, tokens, norm_gain, qkv_weight, out_weight)
        return shards(tokens, norm_gain, qkv_weight, out_weight)

    return jax.shard_map(body, mesh=mesh, in_specs=in_specs, out_specs=out_specs, check_vma=False)
```

profile of v0, /device:TPU:0, one launch (start us, length us, event | category | flops | bytes accessed | tf_op | source)
XLA Modules:
  0.0 101.5 jit_solution(9908469070567574225)
XLA Ops:
  0.0 1.3 %reshape.3.gain_ref = f32[1,1536]{1,0:T(1,128)} reshape(f32[1536]{0:T(1024)} %param.5) | data formatting | bytes 12288 | tf_op jit(solution)/shard_map/reshape | solution.py:380
  1.3 97.8 %shard_map.46 = bf16[384,1536]{1,0:T(8,128)(2,1)} custom-call(bf16[384,1536]{1,0:T(8,128)(2,1)} %tok_hbm.1, f32[1,1536]{1,0:T(1,128)} %reshape.3.gain_ref, bf16[3,1536,1536]{2,1,0:T(8,128)(2,1)} %bitcast.1, bf16[1536,1536]{1,0:T(8,128)(2,1)} %wo_hbm.1), custom_call_target="tpu_custom_call" | custom-call | tf_op jit(solution)/shard_map/pallas_call | solution.py:355
  99.1 2.4 %copy.6 = bf16[384,1536]{1,0:T(8,128)(2,1)} copy(bf16[384,1536]{1,0:T(8,128)(2,1)} %shard_map.46) | data formatting | bytes 2359296
where the time goes:
time: 102 us; the launch traced here: 101 us
  Pallas kernels  97.8 us (96%)
  local copies, waits for them, and re-layouts  3.65 us (4%)
    pallas_call x1, Pallas kernels, fused_shards(): pl.pallas_call(functools.partial(sublayer_kernel, rows_n, cols_n), out_sh...  97.8 us
    unnamed x1, local copies, waits for them, and re-layouts  2.36 us

commit v1 on v0

--- a/solution.py
+++ b/solution.py
@@ -61,32 +61,35 @@
 
 MESH = pl.DeviceIdType.MESH
 WIDE = 2 * K
-SKEW = 1
 ROWS = 32
 PIECE = 128
-PARTS = 2
 
 
 def sublayer_kernel(
-    rows_n, cols_n, tok_hbm, gain_ref, w_hbm, wo_hbm, out_ref,
-    tok, wide_w, stat_col, stats, normed, arrived, summed, attended, late_w,
-    tok_sem, w_sem, late_sem, st_send, st_recv, rs_send, rs_recv, at_send, at_recv,
-    lw_send, lw_recv, fw_send, fw_recv, la_send, la_recv,
+    rows_n, dp_n, tok_hbm, gain_ref, w_hbm, wo_hbm, out_hbm,
+    tok, wide_w, gain_row, stat_col, stats, normed, arrived, summed, attended, late_w, total, out,
+    tok_sem, w_sem, late_sem, out_sem, st_send, st_recv, rs_send, rs_recv, at_send, at_recv,
+    la_send, la_recv, lx_send, lx_recv, ly_send, ly_recv, lc_send, lc_recv, ld_send, ld_recv,
 ):
     z = lax.axis_index("row")
     col = lax.axis_index("col")
+    dp = lax.axis_index("dp")
     tokens_n, block = tok.shape
     half = w_hbm.shape[2] // 2
     pairs = half // WIDE
     chunks = 3 * pairs
     tiles = block // WIDE
     pieces = tokens_n // PIECE
-    part_rows = tokens_n // PARTS
+    quarter = WIDE // dp_n
     partner = {"col": 1 - col}
+    sibling_at = dp + 1 - 2 * (dp % 2)
+    across_at = (dp + 2) % dp_n
+    sibling, across = {"dp": sibling_at}, {"dp": across_at}
     scaling = 1.0 / math.sqrt(K)
+    last_place = rows_n - 1
 
     def weight_copy(d, c):
-        pair, kind = c // 3, c % 3
+        pair, kind = c // 3, (c + 1) % 3
         first = pl.multiple_of(d * half + pair * WIDE, WIDE)
         return pltpu.make_async_copy(
             w_hbm.at[kind, :, pl.ds(first, WIDE)], wide_w.at[d, c], w_sem.at[d, c]
@@ -100,30 +103,37 @@
         weight_copy(0, c).start()
         weight_copy(1, c).start()
 
-    dp = lax.axis_index("dp")
-    side = dp % 2
-    sibling = {"dp": dp + 1 - 2 * side}
-    split = WIDE // 2
-
     def own_copy(d, p):
         rows = pl.ds(d * half + p * WIDE, WIDE)
         return pltpu.make_async_copy(wo_hbm.at[rows], late_w.at[col, d, p], late_sem.at[d, p])
 
+    def quarter_at(which):
+        return pl.ds(pl.multiple_of(which * quarter, quarter), quarter)
+
     def share_copy(d, p, owner):
-        first = pl.multiple_of(d * half + p * WIDE + side * split, split)
-        at = pl.ds(pl.multiple_of(side * split, split), split)
-        return pltpu.make_async_remote_copy(
-            src_ref=wo_hbm.at[pl.ds(first, split)], dst_ref=late_w.at[owner, d, p, at],
-            send_sem=lw_send.at[d, p], recv_sem=lw_recv.at[d, p], device_id=partner,
+        first = pl.multiple_of(d * half + p * WIDE + dp * quarter, quarter)
+        return pltpu.make_async_remote_copy(
+            src_ref=wo_hbm.at[pl.ds(first, quarter)],
+            dst_ref=late_w.at[owner, d, p, quarter_at(dp)],
+            send_sem=lx_send.at[d, p], recv_sem=lx_recv.at[d, p], device_id=partner,
             device_id_type=MESH,
         )
 
-    def hand_copy(d, p, which):
-        piece = late_w.at[1 - col, d, p, pl.ds(pl.multiple_of(which * split, split), split)]
-        return pltpu.make_async_remote_copy(
-            src_ref=piece, dst_ref=piece, send_sem=fw_send.at[d, p],
-            recv_sem=fw_recv.at[d, p], device_id=sibling, device_id_type=MESH,
-        )
+    def pass_copy(d, p, which, sends, recvs, device):
+        piece = late_w.at[1 - col, d, p, quarter_at(which)]
+        return pltpu.make_async_remote_copy(
+            src_ref=piece, dst_ref=piece, send_sem=sends.at[d, p], recv_sem=recvs.at[d, p],
+            device_id=device, device_id_type=MESH,
+        )
+
+    def across_copy(d, p, which):
+        return pass_copy(d, p, which, ly_send, ly_recv, across)
+
+    def near_copy(d, p, which):
+        return pass_copy(d, p, which, lc_send, lc_recv, sibling)
+
+    def far_copy(d, p, which):
+        return pass_copy(d, p, which, ld_send, ld_recv, sibling)
 
     blocks = [(d, p) for p in range(pairs) for d in range(2)]
     for d, p in blocks:
@@ -134,9 +144,11 @@
         pl.semaphore_signal(
             barrier, inc=1, device_id={"row": lax.rem(z + o, rows_n)}, device_id_type=MESH
         )
-    pl.semaphore_signal(barrier, inc=1, device_id=partner, device_id_type=MESH)
-    pl.semaphore_signal(barrier, inc=1, device_id=sibling, device_id_type=MESH)
-
+    for device in (partner, sibling, across):
+        pl.semaphore_signal(barrier, inc=1, device_id=device, device_id_type=MESH)
+
+    for j in range(block // 128):
+        gain_row[0:1, j * 128:(j + 1) * 128] = gain_ref[j:j + 1, :]
     tok_copy.wait()
 
     @pl.loop(0, tokens_n // ROWS)
@@ -151,7 +163,7 @@
 
     stats[z, 0] = stat_col[0].T[0:8]
     stats[z, 1] = stat_col[1].T[0:8]
-    pl.semaphore_wait(barrier, rows_n + 1)
+    pl.semaphore_wait(barrier, rows_n + 2)
 
     def stat_copy(o):
         return pltpu.make_async_remote_copy(
@@ -187,19 +199,19 @@
         at = pl.ds(pl.multiple_of(i * ROWS, ROWS), ROWS)
         x = tok[at, :].astype(jnp.float32)
         away = (x - stat_col[0, at, 0:1]) * stat_col[1, at, 0:1]
-        normed[at, :] = (away * gain_ref[...]).astype(jnp.bfloat16)
+        normed[at, :] = (away * gain_row[...]).astype(jnp.bfloat16)
 
     def place(d):
-        return z if d == 1 else rows_n - 1 - z
+        return z if d == 1 else last_place - z
 
     def onward(d):
-        return {"row": jnp.clip(z + 1 if d == 1 else z - 1, 0, rows_n - 1)}
+        return {"row": jnp.clip(z + 1 if d == 1 else z - 1, 0, last_place)}
 
     def back(d):
-        return {"row": jnp.clip(z - 1 if d == 1 else z + 1, 0, rows_n - 1)}
+        return {"row": jnp.clip(z - 1 if d == 1 else z + 1, 0, last_place)}
 
     def sum_copy(d, c, i):
-        at = pl.ds(i * part_rows, part_rows)
+        at = pl.ds(i * PIECE, PIECE)
         return pltpu.make_async_remote_copy(
             src_ref=summed.at[d, c, at], dst_ref=arrived.at[d, c, at],
             send_sem=rs_send.at[d, c, i], recv_sem=rs_recv.at[d, c, i],
@@ -224,9 +236,9 @@
         rows = pl.ds(i * PIECE, PIECE)
         for h in range(2):
             at = slice(h * K, (h + 1) * K)
-            q = summed[d, 3 * p, rows, at]
-            k = summed[d, 3 * p + 1, :, at]
-            v = summed[d, 3 * p + 2, :, at]
+            k = summed[d, 3 * p, :, at]
+            v = summed[d, 3 * p + 1, :, at]
+            q = summed[d, 3 * p + 2, rows, at]
             scores = lax.dot_general(
                 q, k, (((1,), (1,)), ((), ())), preferred_element_type=jnp.float32
             ) * scaling
@@ -236,25 +248,38 @@
                 weights.astype(jnp.bfloat16), v, preferred_element_type=jnp.float32
             ).astype(jnp.bfloat16)
 
-    last_place = rows_n - 1
-    slots = chunks + 2 * SKEW * last_place
-    hand_slots = [min(4 + 2 * b, slots - 1) for b in range(len(blocks))]
+    def weights_ready(p):
+        for d in range(2):
+            own_copy(d, p).wait()
+            near_copy(d, p, sibling_at).wait_recv()
+            far_copy(d, p, (sibling_at + 2) % dp_n).wait_recv()
+
+    def fold(p, rows, at):
+        return sum(
+            jnp.dot(
+                attended[owner, d, p, rows], late_w[owner, d, p, :, at],
+                preferred_element_type=jnp.float32,
+            )
+            for owner in range(2) for d in range(2)
+        )
+
+    slots = chunks + 2 * last_place
+    every = pl.ds(0, tokens_n)
 
     @pl.loop(0, slots)
     def _(t):
         for d in range(2):
             pos = place(d)
-            c = t - SKEW * pos
+            c = t - pos
 
             @pl.when((c >= 0) & (c < chunks))
             def _():
                 weight_copy(d, c).wait()
                 part = jnp.dot(normed[...], wide_w[d, c], preferred_element_type=jnp.float32)
 
-                for i in range(PARTS):
-                    lo = i * part_rows
-                    at = pl.ds(lo, part_rows)
-                    share = part[lo:lo + part_rows]
+                for i in range(pieces):
+                    at = pl.ds(i * PIECE, PIECE)
+                    share = part[i * PIECE:(i + 1) * PIECE]
 
                     @pl.when(pos == 0)
                     def _():
@@ -263,28 +288,28 @@
                     @pl.when(pos > 0)
                     def _():
                         sum_copy(d, c, i).wait_recv()
-                        total = share + arrived[d, c, at].astype(jnp.float32)
-                        summed[d, c, at] = total.astype(jnp.bfloat16)
+                        whole = share + arrived[d, c, at].astype(jnp.float32)
+                        summed[d, c, at] = whole.astype(jnp.bfloat16)
 
                     @pl.when(pos < last_place)
                     def _():
                         sum_copy(d, c, i).start()
 
+                    @pl.when((pos == last_place) & (c % 3 == 2))
+                    def _():
+                        attend_piece(d, c // 3, i)
+                        attended_copy(d, c // 3, i).start()
+                        cross_copy(d, c // 3, i, col).start()
+
         for d in range(2):
             pos = place(d)
-            e = t - SKEW * last_place - SKEW * (last_place - pos)
+            e = t - last_place - (last_place - pos)
             p = e // 3
 
-            @pl.when((e >= 0) & (e < chunks) & (e % 3 == 2))
+            @pl.when((pos < last_place) & (e >= 0) & (e < chunks) & (e % 3 == 2))
             def _():
                 for i in range(pieces):
-                    @pl.when(pos == last_place)
-                    def _():
-                        attend_piece(d, p, i)
-
-                    @pl.when(pos < last_place)
-                    def _():
-                        attended_copy(d, p, i).wait_recv()
+                    attended_copy(d, p, i).wait_recv()
 
                     @pl.when(pos > 0)
                     def _():
@@ -292,29 +317,52 @@
 
                     cross_copy(d, p, i, col).start()
 
-        for (d, p), slot in zip(blocks, hand_slots):
-            @pl.when(t == slot)
+        for b, (d, p) in enumerate(blocks):
+            @pl.when(t == min(b + 2, slots - 1))
             def _():
                 share_copy(d, p, 1 - col).wait_recv()
-                hand_copy(d, p, side).start()
-
-    for d, p in blocks:
-        own_copy(d, p).wait()
-        hand_copy(d, p, 1 - side).wait_recv()
-        for i in range(pieces):
-            cross_copy(d, p, i, 1 - col).wait_recv()
-
-    @pl.loop(0, tiles)
-    def _(j):
-        at = pl.ds(pl.multiple_of(j * WIDE, WIDE), WIDE)
-        total = jnp.zeros((tokens_n, WIDE), jnp.float32)
-        for owner in range(2):
-            for d, p in blocks:
-                total = total + jnp.dot(
-                    attended[owner, d, p], late_w[owner, d, p, :, at],
-                    preferred_element_type=jnp.float32,
-                )
-        out_ref[:, at] = total.astype(jnp.bfloat16)
+                across_copy(d, p, dp).start()
+                near_copy(d, p, dp).start()
+
+            @pl.when(t == min(b + 5, slots - 1))
+            def _():
+                across_copy(d, p, across_at).wait_recv()
+                far_copy(d, p, across_at).start()
+
+        for p in range(pairs - 1):
+            @pl.when(t == 3 * p + 3 + 2 * last_place)
+            def _():
+                weights_ready(p)
+                for d in range(2):
+                    for i in range(pieces):
+                        cross_copy(d, p, i, 1 - col).wait_recv()
+
+                @pl.loop(0, tiles)
+                def _(j):
+                    at = pl.ds(pl.multiple_of(j * WIDE, WIDE), WIDE)
+                    if p == 0:
+                        total[:, at] = fold(p, every, at)
+                    else:
+                        total[:, at] = total[:, at] + fold(p, every, at)
+
+    final = pairs - 1
+    weights_ready(final)
+
+    def out_copy(i):
+        rows = pl.ds(i * PIECE, PIECE)
+        return pltpu.make_async_copy(out.at[rows], out_hbm.at[rows], out_sem.at[i])
+
+    for i in range(pieces):
+        rows = pl.ds(i * PIECE, PIECE)
+        for d in range(2):
+            cross_copy(d, final, i, 1 - col).wait_recv()
+
+        @pl.loop(0, tiles)
+        def _(j):
+            at = pl.ds(pl.multiple_of(j * WIDE, WIDE), WIDE)
+            out[rows, at] = (total[rows, at] + fold(final, rows, at)).astype(jnp.bfloat16)
+
+        out_copy(i).start()
 
     for o in range(1, rows_n):
         stat_copy(o).wait_send()
@@ -325,7 +373,7 @@
         def _():
             @pl.loop(0, chunks)
             def _(c):
-                for i in range(PARTS):
+                for i in range(pieces):
                     sum_copy(d, c, i).wait_send()
 
         @pl.when(pos > 0)
@@ -337,12 +385,16 @@
 
     for d, p in blocks:
         share_copy(d, p, col).wait_send()
-        hand_copy(d, p, side).wait_send()
+        across_copy(d, p, dp).wait_send()
+        near_copy(d, p, dp).wait_send()
+        far_copy(d, p, across_at).wait_send()
         for i in range(pieces):
             cross_copy(d, p, i, col).wait_send()
-
-
-def fused_shards(rows_n, cols_n, tokens, norm_gain, qkv_weight, out_weight):
+    for i in range(pieces):
+        out_copy(i).wait()
+
+
+def fused_shards(rows_n, dp_n, tokens, norm_gain, qkv_weight, out_weight):
     tokens_n, block = tokens.shape
     head_columns = qkv_weight.shape[2]
     pairs = head_columns // (2 * WIDE)
@@ -353,13 +405,14 @@
     dma = pltpu.SemaphoreType.DMA
     bf16, f32 = jnp.bfloat16, jnp.float32
     return pl.pallas_call(
-        functools.partial(sublayer_kernel, rows_n, cols_n),
+        functools.partial(sublayer_kernel, rows_n, dp_n),
         out_shape=jax.ShapeDtypeStruct((tokens_n, block), bf16),
         in_specs=[any_space, vmem, any_space, any_space],
-        out_specs=vmem,
+        out_specs=any_space,
         scratch_shapes=[
             pltpu.VMEM((tokens_n, block), bf16),
             pltpu.VMEM((2, chunks, block, WIDE), bf16),
+            pltpu.VMEM((1, block), f32),
             pltpu.VMEM((2, tokens_n, 128), f32),
             pltpu.VMEM((rows_n, 2, 8, tokens_n), f32),
             pltpu.VMEM((tokens_n, block), bf16),
@@ -367,33 +420,39 @@
             pltpu.VMEM((2, chunks, tokens_n, WIDE), bf16),
             pltpu.VMEM((2, 2, pairs, tokens_n, WIDE), bf16),
             pltpu.VMEM((2, 2, pairs, WIDE, block), bf16),
-            dma, dma((2, chunks)), dma((2, pairs)),
+            pltpu.VMEM((tokens_n, block), f32),
+            pltpu.VMEM((tokens_n, block), bf16),
+            dma, dma((2, chunks)), dma((2, pairs)), dma((pieces,)),
             dma((rows_n,)), dma((rows_n,)),
-            dma((2, chunks, PARTS)), dma((2, chunks, PARTS)),
+            dma((2, chunks, pieces)), dma((2, chunks, pieces)),
+            dma((2, pairs, pieces)), dma((2, pairs, pieces)),
             dma((2, pairs, pieces)), dma((2, pairs, pieces)),
             dma((2, pairs)), dma((2, pairs)), dma((2, pairs)), dma((2, pairs)),
-            dma((2, pairs, pieces)), dma((2, pairs, pieces)),
+            dma((2, pairs)), dma((2, pairs)), dma((2, pairs)), dma((2, pairs)),
         ],
         compiler_params=pltpu.CompilerParams(
-            collective_id=0, has_side_effects=True, vmem_limit_bytes=60 * 1024 * 1024
+            collective_id=0, has_side_effects=True, vmem_limit_bytes=52 * 1024 * 1024
         ),
-    )(tokens, norm_gain.reshape(1, block), jnp.transpose(qkv_weight, (1, 0, 2)), out_weight)
+    )(
+        tokens, norm_gain.reshape(block // 128, 128), jnp.transpose(qkv_weight, (1, 0, 2)),
+        out_weight,
+    )
 
 
 def solution(mesh):
     in_specs = (P("dp", "row"), P("row"), P("row", None, "col"), P("col", "row"))
     out_specs = P("dp", "row")
-    rows_n, cols_n = mesh.shape["row"], mesh.shape["col"]
+    rows_n, cols_n, dp_n = mesh.shape["row"], mesh.shape["col"], mesh.shape["dp"]
 
     def body(tokens, norm_gain, qkv_weight, out_weight):
         tokens_n, block = tokens.shape
         fits = (
-            cols_n == 2 and mesh.shape["dp"] % 2 == 0 and rows_n >= 2 and qkv_weight.shape[2] % (2 * WIDE) == 0
+            cols_n == 2 and dp_n == 4 and rows_n >= 2 and qkv_weight.shape[2] % (2 * WIDE) == 0
             and qkv_weight.shape[2] >= 4 * WIDE
-            and block % WIDE == 0 and tokens_n % 128 == 0
+            and block % WIDE == 0 and tokens_n % PIECE == 0
         )
         if fits:
-            return fused_shards(rows_n, cols_n, tokens, norm_gain, qkv_weight, out_weight)
+            return fused_shards(rows_n, dp_n, tokens, norm_gain, qkv_weight, out_weight)
         return shards(tokens, norm_gain, qkv_weight, out_weight)
 
     return jax.shard_map(body, mesh=mesh, in_specs=in_specs, out_specs=out_specs, check_vma=False)

time: 102 us -> 94.1 us (0.923)
  Pallas kernels: 97.8 us -> 92.2 us
  local copies, waits for them, and re-layouts: 3.65 us -> 1.71 us
    pallas_call x1, Pallas kernels: 97.8 us -> 92.2 us  [fused_shards(): pl.pallas_call(functools.partial(sublayer_kernel, rows_n, dp_n), out_shap...]
    reshape x1 -> x0, local copies, waits for them, and re-layouts: 1.29 us -> none  [fused_shards(): norm_gain.reshape(1, block)]
    unnamed x1 -> x3, local copies, waits for them, and re-layouts: 2.36 us -> 1.71 us
where the time goes in v1:
time: 94.1 us; the launch traced here: 93.9 us
  Pallas kernels  92.2 us (98%)
  local copies, waits for them, and re-layouts  1.71 us (2%)
    pallas_call x1, Pallas kernels, fused_shards(): pl.pallas_call(functools.partial(sublayer_kernel, rows_n, dp_n), out_shap...  92.2 us

profile of v1, /device:TPU:0, one launch (start us, length us, event | category | flops | bytes accessed | tf_op | source)
XLA Modules:
  0.0 93.9 jit_solution(17933483454637423337)
XLA Ops:
  0.0 0.0 copy-start
  0.0 0.7 copy-done
  0.7 92.2 %shard_map.46 = bf16[384,1536]{1,0:T(8,128)(2,1)S(1)} custom-call(bf16[384,1536]{1,0:T(8,128)(2,1)} %tok_hbm.1, f32[12,128]{1,0:T(8,128)S(1)} %bitcast.2, bf16[3,1536,1536]{2,1,0:T(8,128)(2,1)} %bitcast.3, bf16[1536,1536]{1,0:T(8,128)(2,1)} %wo_hbm.1), custom_call_target="tpu_custom_call" | custom-call | tf_op jit(solution)/shard_map/pallas_call | solution.py:407
  92.9 1.0 %copy.6 = bf16[384,1536]{1,0:T(8,128)(2,1)} copy(bf16[384,1536]{1,0:T(8,128)(2,1)S(1)} %shard_map.46) | data formatting | bytes 2359296
Async XLA Ops:
  0.0 0.7 copy-start

commit v2 on v1

v2 whole, which is shorter than its diff:
```python
import functools
import math

import jax
import jax.numpy as jnp
from jax import lax
from jax.experimental import pallas as pl
from jax.experimental.pallas import tpu as pltpu
from jax.sharding import PartitionSpec as P

K = 128


EPSILON = 1e-05


def attend(queries, key_rows, value_rows):
    query_total = queries.shape[0]
    head_count = queries.shape[1] // K
    scaling = 1.0 / math.sqrt(K)
    split_keys = key_rows.reshape(key_rows.shape[0], head_count, K)
    split_values = value_rows.reshape(value_rows.shape[0], head_count, K)
    split_queries = queries.reshape(query_total, head_count, K)
    scores = (
        jnp.einsum("qhd,khd->hqk", split_queries, split_keys, preferred_element_type=jnp.float32)
        * scaling
    )
    largest = jnp.max(scores, axis=2, keepdims=True)
    exponent = jnp.exp(scores - largest)
    softmax_weights = (exponent / jnp.sum(exponent, axis=2, keepdims=True)).astype(jnp.bfloat16)
    mixed = jnp.einsum(
        "hqk,khd->qhd", softmax_weights, split_values, preferred_element_type=jnp.float32
    )
    result = mixed.astype(jnp.bfloat16)
    return result.reshape(query_total, head_count * K)


def shards(tokens, norm_gain, qkv_weight, out_weight):
    row_count, block_width = tokens.shape
    full_width = block_width * lax.axis_size("row")
    values = tokens.astype(jnp.float32)
    totals, squares = lax.psum(
        (jnp.sum(values, axis=1, keepdims=True), jnp.sum(values * values, axis=1, keepdims=True)),
        "row",
    )
    average = totals / full_width
    variance = squares / full_width - average * average
    centered = values - average
    normed = (centered * lax.rsqrt(variance + EPSILON) * norm_gain).astype(jnp.bfloat16)
    head_columns = qkv_weight.shape[2]
    partial_value = jnp.dot(
        normed,
        qkv_weight.reshape(block_width, 3 * head_columns),
        preferred_element_type=jnp.float32,
    )
    summed = lax.psum(partial_value.astype(jnp.bfloat16), "row").reshape(row_count, 3, head_columns)
    attended = attend(summed[:, 0], summed[:, 1], summed[:, 2])
    partial_out = jnp.dot(attended, out_weight, preferred_element_type=jnp.float32)
    return lax.psum(partial_out.astype(jnp.bfloat16), "col")


MESH = pl.DeviceIdType.MESH
WIDE = 2 * K
ROWS = 32
EXTRA = 16
PIECE = 96
SPAN = 1
SKEW = 3
LEAD = 2
RETURN = 6
HAND = 12
HAND_ON = 24


def sublayer_kernel(
    rows_n, dp_n, tok_hbm, gain_hbm, w_hbm, wo_hbm, out,
    tok, wide_w, gain_ref, gain_row, stat_col, stats, spread_col, normed, part, gain_sum, gain_all,
    arrived, summed, attended, late_w, total,
    tok_sem, gain_sem, w_sem, late_sem, st_send, st_recv, gs_send, gs_recv, rs_send, rs_recv,
    at_send, at_recv, di_send, la_send, la_recv, lx_send, lx_recv, ly_send, ly_recv, lc_send, lc_recv,
    ld_send, ld_recv,
):
    z = lax.axis_index("row")
    col = lax.axis_index("col")
    dp = lax.axis_index("dp")
    tokens_n, block = tok.shape
    half = w_hbm.shape[2] // 2
    pairs = half // WIDE
    chunks = 3 * pairs
    pieces = tokens_n // PIECE
    units = chunks * pieces
    span = SPAN * PIECE
    spans = tokens_n // span
    tiles = block // WIDE
    quarter = WIDE // dp_n
    partner = {"col": 1 - col}
    sibling_at = dp + 1 - 2 * (dp % 2)
    across_at = (dp + 2) % dp_n
    sibling, across = {"dp": sibling_at}, {"dp": across_at}
    scaling = 1.0 / math.sqrt(K)
    last_place = rows_n - 1
    f32, bf16 = jnp.float32, jnp.bfloat16

    def weight_copy(d, c):
        pair, kind = c // 3, (c + 1) % 3
        first = pl.multiple_of(d * half + pair * WIDE, WIDE)
        return pltpu.make_async_copy(
            w_hbm.at[kind, :, pl.ds(first, WIDE)], wide_w.at[d, c], w_sem.at[d, c]
        )

    gain_load = pltpu.make_async_copy(gain_hbm, gain_ref, gain_sem)
    gain_load.start()

    def tok_copy(i):
        rows = pl.ds(pl.multiple_of(i * PIECE, PIECE), PIECE)
        return pltpu.make_async_copy(tok_hbm.at[rows], tok.at[rows], tok_sem.at[i])

    @pl.loop(0, pieces)
    def _(i):
        tok_copy(i).start()

    @pl.loop(0, chunks)
    def _(c):
        weight_copy(0, c).start()
        weight_copy(1, c).start()

    def head_columns(owner, d):
        return pl.ds(pl.multiple_of((owner * 2 + d) * WIDE, WIDE), WIDE)

    def own_copy(d, p):
        rows = pl.ds(d * half + p * WIDE, WIDE)
        return pltpu.make_async_copy(
            wo_hbm.at[rows], late_w.at[p, head_columns(col, d)], late_sem.at[d, p]
        )

    def quarter_at(owner, d, which):
        first = (owner * 2 + d) * WIDE + which * quarter
        return pl.ds(pl.multiple_of(first, quarter), quarter)

    def share_copy(d, p, owner):
        first = pl.multiple_of(d * half + p * WIDE + dp * quarter, quarter)
        return pltpu.make_async_remote_copy(
            src_ref=wo_hbm.at[pl.ds(first, quarter)],
            dst_ref=late_w.at[p, quarter_at(owner, d, dp)],
            send_sem=lx_send, recv_sem=lx_recv.at[d, p], device_id=partner,
            device_id_type=MESH,
        )

    def pass_copy(d, p, which, sends, recvs, device):
        piece = late_w.at[p, quarter_at(1 - col, d, which)]
        return pltpu.make_async_remote_copy(
            src_ref=piece, dst_ref=piece, send_sem=sends, recv_sem=recvs.at[d, p],
            device_id=device, device_id_type=MESH,
        )

    def across_copy(d, p, which):
        return pass_copy(d, p, which, ly_send, ly_recv, across)

    def near_copy(d, p, which):
        return pass_copy(d, p, which, lc_send, lc_recv, sibling)

    def far_copy(d, p, which):
        return pass_copy(d, p, which, ld_send, ld_recv, sibling)

    blocks = [(d, p) for p in range(pairs) for d in range(2)]
    for d, p in blocks:
        own_copy(d, p).start()

    barrier = pltpu.get_barrier_semaphore()
    for o in range(1, rows_n):
        pl.semaphore_signal(
            barrier, inc=1, device_id={"row": lax.rem(z + o, rows_n)}, device_id_type=MESH
        )
    for device in (partner, sibling, across):
        pl.semaphore_signal(barrier, inc=1, device_id=device, device_id_type=MESH)

    gain_load.wait()
    for j in range(block // 128):
        gain_row[0:1, j * 128:(j + 1) * 128] = gain_ref[j:j + 1, :]
    gain = gain_row[...]
    high = gain.astype(bf16).astype(f32)
    row = lax.broadcasted_iota(jnp.int32, (EXTRA, block), 0)
    normed[pl.ds(tokens_n, EXTRA), :] = jnp.where(
        row == 0, high, jnp.where(row == 1, gain - high, 0.0)
    ).astype(bf16)
    def place(d):
        return jnp.where(d == 1, z, last_place - z)

    def end_of(d):
        return jnp.where(d == 1, last_place, 0)

    def onward(d):
        return {"row": jnp.clip(jnp.where(d == 1, z + 1, z - 1), 0, last_place)}

    def back(d):
        return {"row": jnp.clip(jnp.where(d == 1, z - 1, z + 1), 0, last_place)}

    def stat_copy(which, source):
        return pltpu.make_async_remote_copy(
            src_ref=stats.at[source], dst_ref=stats.at[source], send_sem=st_send.at[which],
            recv_sem=st_recv.at[source], device_id={"row": which * last_place},
            device_id_type=MESH,
        )

    def gain_copy(d, c, source):
        return pltpu.make_async_remote_copy(
            src_ref=gain_sum.at[d, c], dst_ref=gain_all.at[source, c], send_sem=gs_send.at[d],
            recv_sem=gs_recv.at[source, c], device_id={"row": end_of(d)}, device_id_type=MESH,
        )

    def sum_copy(d, c, i):
        at = pl.ds(pl.multiple_of(i * PIECE, PIECE), PIECE)
        return pltpu.make_async_remote_copy(
            src_ref=summed.at[d, c, at], dst_ref=arrived.at[d, c, at],
            send_sem=rs_send.at[d], recv_sem=rs_recv.at[d, c, i],
            device_id=onward(d), device_id_type=MESH,
        )

    def attended_part(owner, d, p, i):
        rows = pl.ds(pl.multiple_of(i * span, span), span)
        return attended.at[p, rows, head_columns(owner, d)]

    def attended_copy(d, p, i):
        piece = attended_part(col, d, p, i)
        return pltpu.make_async_remote_copy(
            src_ref=piece, dst_ref=piece, send_sem=at_send.at[d],
            recv_sem=at_recv.at[d, p, i], device_id=back(d), device_id_type=MESH,
        )

    def direct_copy(d, p, i, o):
        piece = attended_part(col, d, p, i)
        return pltpu.make_async_remote_copy(
            src_ref=piece, dst_ref=piece, send_sem=di_send.at[o],
            recv_sem=at_recv.at[d, p, i],
            device_id={"row": jnp.clip(jnp.where(d == 1, z - o, z + o), 0, last_place)},
            device_id_type=MESH,
        )

    def cross_copy(d, p, i, owner):
        piece = attended_part(owner, d, p, i)
        return pltpu.make_async_remote_copy(
            src_ref=piece, dst_ref=piece, send_sem=la_send,
            recv_sem=la_recv.at[d, p, i], device_id=partner, device_id_type=MESH,
        )

    def attend_piece(d, p, i):
        rows = pl.ds(pl.multiple_of(i * span, span), span)
        first = (col * 2 + d) * WIDE
        for h in range(2):
            at = slice(h * K, (h + 1) * K)
            k = summed[d, 3 * p, :, at]
            v = summed[d, 3 * p + 1, :, at]
            q = summed[d, 3 * p + 2, rows, at]
            scores = lax.dot_general(
                q, k, (((1,), (1,)), ((), ())), preferred_element_type=f32
            )
            exponent = jnp.exp2(
                (scores - jnp.max(scores, axis=1, keepdims=True)) * (scaling * math.log2(math.e))
            )
            mixed = jnp.dot(exponent.astype(bf16), v, preferred_element_type=f32)
            attended[p, rows, pl.ds(pl.multiple_of(first + h * K, K), K)] = (
                mixed / jnp.sum(exponent, axis=1, keepdims=True)
            ).astype(bf16)

    def spread_statistics():
        for o in range(1, rows_n):
            stat_copy(0, lax.rem(z + o, rows_n)).wait_recv()
        mean = sum(stats[i, 0] for i in range(rows_n)) * (1.0 / rows_n)
        spread = sum(
            stats[i, 1] * (1.0 / block) + (stats[i, 0] - mean) * (stats[i, 0] - mean)
            for i in range(rows_n)
        ) * (1.0 / rows_n)
        scale = lax.rsqrt(spread + EPSILON)
        for i in range(rows_n):
            shift = (stats[i, 0] - mean) * scale
            spread_col[i] = jnp.broadcast_to(shift, (128, tokens_n)).T
        spread_col[rows_n] = jnp.broadcast_to(scale, (128, tokens_n)).T

    def weights_ready(p):
        for d in range(2):
            own_copy(d, p).wait()
            near_copy(d, p, sibling_at).wait_recv()
            far_copy(d, p, (sibling_at + 2) % dp_n).wait_recv()

    def pair_ready(p):
        weights_ready(p)
        for d in range(2):
            for i in range(spans):
                cross_copy(d, p, i, 1 - col).wait_recv()

    def fold(p, rows, at):
        return jnp.dot(attended[p, rows, :], late_w[p, :, at], preferred_element_type=f32)

    nearer = jnp.where(z < last_place - z, 1, 0)
    starts = (z == 0) | (z == last_place)

    def centre(i):
        tok_copy(i).wait()

        @pl.loop(0, PIECE // ROWS)
        def _(j):
            at = pl.ds(pl.multiple_of(i * PIECE + j * ROWS, ROWS), ROWS)
            x = tok[at, :].astype(f32)
            mean = jnp.sum(x, axis=1, keepdims=True) * (1.0 / block)
            away = x - mean
            square = jnp.sum(away * away, axis=1, keepdims=True)
            normed[at, :] = (away * gain_row[...]).astype(bf16)
            stat_col[0, at, :] = jnp.broadcast_to(mean, (ROWS, 128))
            stat_col[1, at, :] = jnp.broadcast_to(square, (ROWS, 128))

    def first_piece(i):
        rows = pl.ds(pl.multiple_of(i * PIECE, PIECE), PIECE)
        summed[nearer, 0, rows] = jnp.dot(
            normed[rows, :], wide_w[nearer, 0], preferred_element_type=f32
        ).astype(bf16)

    centre(0)

    @pl.when(starts)
    def _():
        weight_copy(nearer, 0).wait()
        first_piece(0)

    pl.semaphore_wait(barrier, rows_n + 2)

    @pl.when(starts)
    def _():
        sum_copy(nearer, 0, 0).start()

    @pl.loop(0, pairs)
    def _(p):
        share_copy(0, p, col).start()
        share_copy(1, p, col).start()

    @pl.loop(1, pieces)
    def _(i):
        centre(i)

        @pl.when(starts)
        def _():
            first_piece(i)
            sum_copy(nearer, 0, i).start()

    @pl.when(starts)
    def _():
        value = jnp.dot(
            normed[pl.ds(tokens_n, EXTRA), :], wide_w[nearer, 0], preferred_element_type=f32
        )
        gain_sum[nearer, 0] = value[0:1] + value[1:2]
        gain_copy(nearer, 0, z).start()

    def offset(pos):
        return jnp.where(pos > 0, LEAD + SKEW * pos, -pieces)

    end_offset = LEAD + SKEW * last_place
    slots = units + end_offset + RETURN + SKEW * last_place
    every = pl.ds(0, tokens_n)

    def fold_pair(p):
        pair_ready(p)
        for j in range(tiles // 2):
            at = slice(j * 2 * WIDE, (j + 1) * 2 * WIDE)
            value = fold(p, every, at)
            total[:, at] = value if p == 0 else total[:, at] + value

    stat_slot = jnp.where(starts, 0, LEAD + SKEW + 1)

    @pl.loop(0, slots)
    def _(t):
        @pl.when(t == stat_slot)
        def _():
            stats[z, 0] = stat_col[0].T[0:1]
            stats[z, 1] = stat_col[1].T[0:1]
            for which in range(2):
                @pl.when(z != which * last_place)
                def _():
                    stat_copy(which, z).start()

        @pl.when((t == end_offset - 1) & starts)
        def _():
            spread_statistics()

        for k in range(2):
            d = nearer if k == 0 else 1 - nearer
            pos = place(d)
            u = t - offset(pos)
            c, i = u // pieces, u % pieces

            @pl.when((u >= 0) & (u < units))
            def _():
                rows = pl.ds(pl.multiple_of(i * PIECE, PIECE), PIECE)

                @pl.when(i == 0)
                def _():
                    weight_copy(d, c).wait()
                    value = jnp.dot(normed[...], wide_w[d, c], preferred_element_type=f32)
                    part[d] = value[0:tokens_n]
                    gain_value = value[tokens_n:tokens_n + 1] + value[tokens_n + 1:tokens_n + 2]

                    @pl.when(pos < last_place)
                    def _():
                        gain_sum[d, c] = gain_value
                        gain_copy(d, c, z).start()

                    @pl.when(pos == last_place)
                    def _():
                        gain_all[z, c] = gain_value
                        for o in range(1, rows_n):
                            gain_copy(d, c, lax.rem(z + o, rows_n)).wait_recv()

                @pl.when(pos == 0)
                def _():
                    summed[d, c, rows] = part[d, rows].astype(bf16)

                @pl.when(pos > 0)
                def _():
                    sum_copy(d, c, i).wait_recv()

                @pl.when((pos > 0) & (pos < last_place))
                def _():
                    summed[d, c, rows] = (part[d, rows] + arrived[d, c, rows].astype(f32)).astype(bf16)

                @pl.when(pos < last_place)
                def _():
                    sum_copy(d, c, i).start()

                @pl.when(pos == last_place)
                def _():
                    scale = spread_col[rows_n, rows]
                    for h in range(2):
                        lanes = slice(h * 128, (h + 1) * 128)
                        whole = part[d, rows, lanes] + arrived[d, c, rows, lanes].astype(f32)
                        whole = whole * scale
                        for source in range(rows_n):
                            whole = whole + spread_col[source, rows] * gain_all[source, c, :, lanes]
                        summed[d, c, rows, lanes] = whole.astype(bf16)

                @pl.when((pos == last_place) & (c % 3 == 2) & (i % SPAN == SPAN - 1))
                def _():
                    p, s = c // 3, i // SPAN
                    attend_piece(d, p, s)

                    @pl.when(u < units - 1)
                    def _():
                        attended_copy(d, p, s).start()

                    @pl.when(u == units - 1)
                    def _():
                        for o in range(last_place, 0, -1):
                            direct_copy(d, p, s, o).start()

                    cross_copy(d, p, s, col).start()

        for k in range(2):
            d = 1 - nearer if k == 0 else nearer
            pos = place(d)
            u = t - end_offset - RETURN - SKEW * (last_place - pos)
            c, i = u // pieces, u % pieces
            p = c // 3

            @pl.when(
                (pos < last_place) & (u >= 0) & (u < units) & (c % 3 == 2) & (i % SPAN == SPAN - 1)
            )
            def _():
                s = i // SPAN
                attended_copy(d, p, s).wait_recv()

                @pl.when((pos > 0) & (u < units - 1))
                def _():
                    attended_copy(d, p, s).start()

                cross_copy(d, p, s, col).start()

        @pl.when((t >= HAND) & (t < HAND + pieces * len(blocks)) & ((t - HAND) % pieces == 0))
        def _():
            b = (t - HAND) // pieces
            d, p = b % 2, b // 2
            share_copy(d, p, 1 - col).wait_recv()
            across_copy(d, p, dp).start()
            near_copy(d, p, dp).start()

        @pl.when(
            (t >= HAND_ON) & (t < HAND_ON + pieces * len(blocks)) & ((t - HAND_ON) % pieces == 0)
        )
        def _():
            b = (t - HAND_ON) // pieces
            d, p = b % 2, b // 2
            across_copy(d, p, across_at).wait_recv()
            far_copy(d, p, across_at).start()

        @pl.when(t == units + end_offset)
        def _():
            for p in range(pairs - 2):
                fold_pair(p)

    final = pairs - 1
    fold_pair(final - 1)
    weights_ready(final)

    for i in range(spans):
        rows = pl.ds(i * span, span)
        for d in range(2):
            cross_copy(d, final, i, 1 - col).wait_recv()
        for j in range(tiles // 2):
            at = slice(j * 2 * WIDE, (j + 1) * 2 * WIDE)
            out[rows, at] = (total[rows, at] + fold(final, rows, at)).astype(bf16)

    def sent(source, sem):
        pltpu.make_async_remote_copy(
            src_ref=source, dst_ref=source, send_sem=sem, recv_sem=lx_recv.at[0, 0],
            device_id=partner, device_id_type=MESH,
        ).wait_send()

    for which in range(2):
        @pl.when(z != which * last_place)
        def _():
            stat_copy(which, z).wait_send()
    for d in range(2):
        pos = place(d)

        @pl.when(pos < last_place)
        def _():
            sent(gain_sum.at[d], gs_send.at[d])
            sent(summed.at[d], rs_send.at[d])

        @pl.when(pos > 0)
        def _():
            sent(wide_w.at[0, 0, pl.ds(0, pairs * tokens_n - span)], at_send.at[d])

        @pl.when(pos == last_place)
        def _():
            for o in range(1, rows_n):
                direct_copy(d, final, spans - 1, o).wait_send()

    sent(summed.at[0, pl.ds(0, 2 * pairs)], la_send)
    for sem in (lx_send, ly_send, lc_send, ld_send):
        sent(late_w.at[0, pl.ds(0, 2 * pairs * quarter)], sem)


def fused_shards(rows_n, dp_n, tokens, norm_gain, qkv_weight, out_weight):
    tokens_n, block = tokens.shape
    pairs = qkv_weight.shape[2] // (2 * WIDE)
    chunks = 3 * pairs
    pieces, spans = tokens_n // PIECE, tokens_n // (SPAN * PIECE)
    any_space = pl.BlockSpec(memory_space=pl.ANY)
    vmem = pl.BlockSpec(memory_space=pltpu.VMEM)
    hbm = pl.BlockSpec(memory_space=pltpu.HBM)
    dma = pltpu.SemaphoreType.DMA
    bf16, f32 = jnp.bfloat16, jnp.float32
    return pl.pallas_call(
        functools.partial(sublayer_kernel, rows_n, dp_n),
        out_shape=pltpu.VMEM((tokens_n, block), bf16),
        in_specs=[any_space, hbm, any_space, any_space],
        out_specs=vmem,
        scratch_shapes=[
            pltpu.VMEM((tokens_n, block), bf16),
            pltpu.VMEM((2, chunks, block, WIDE), bf16),
            pltpu.VMEM((block // 128, 128), f32),
            pltpu.VMEM((1, block), f32),
            pltpu.VMEM((2, tokens_n, 128), f32),
            pltpu.VMEM((rows_n, 2, 1, tokens_n), f32),
            pltpu.VMEM((rows_n + 1, tokens_n, 128), f32),
            pltpu.VMEM((tokens_n + EXTRA, block), bf16),
            pltpu.VMEM((2, tokens_n, WIDE), f32),
            pltpu.VMEM((2, chunks, 1, WIDE), f32),
            pltpu.VMEM((rows_n, chunks, 1, WIDE), f32),
            pltpu.VMEM((2, chunks, tokens_n, WIDE), bf16),
            pltpu.VMEM((2, chunks, tokens_n, WIDE), bf16),
            pltpu.VMEM((pairs, tokens_n, 4 * WIDE), bf16),
            pltpu.VMEM((pairs, 4 * WIDE, block), bf16),
            pltpu.VMEM((tokens_n, block), f32),
            dma((pieces,)), dma, dma((2, chunks)), dma((2, pairs)),
            dma((2,)), dma((rows_n,)), dma((2,)), dma((rows_n, chunks)),
            dma((2,)), dma((2, chunks, pieces)),
            dma((2,)), dma((2, pairs, spans)), dma((rows_n,)),
            dma, dma((2, pairs, spans)),
            dma, dma((2, pairs)), dma, dma((2, pairs)),
            dma, dma((2, pairs)), dma, dma((2, pairs)),
        ],
        compiler_params=pltpu.CompilerParams(
            collective_id=0, has_side_effects=True, vmem_limit_bytes=65800000
        ),
    )(
        tokens, norm_gain.reshape(block // 128, 128), jnp.transpose(qkv_weight, (1, 0, 2)),
        out_weight,
    )


def solution(mesh):
    in_specs = (P("dp", "row"), P("row"), P("row", None, "col"), P("col", "row"))
    out_specs = P("dp", "row")
    rows_n, cols_n, dp_n = mesh.shape["row"], mesh.shape["col"], mesh.shape["dp"]

    def body(tokens, norm_gain, qkv_weight, out_weight):
        tokens_n, block = tokens.shape
        fits = (
            cols_n == 2 and dp_n == 4 and rows_n >= 2 and qkv_weight.shape[2] % (2 * WIDE) == 0
            and qkv_weight.shape[2] >= 4 * WIDE
            and block % (2 * WIDE) == 0 and tokens_n % (SPAN * PIECE) == 0
            and (qkv_weight.shape[2] // (2 * WIDE)) * tokens_n <= block
        )
        if fits:
            return fused_shards(rows_n, dp_n, tokens, norm_gain, qkv_weight, out_weight)
        return shards(tokens, norm_gain, qkv_weight, out_weight)

    return jax.shard_map(body, mesh=mesh, in_specs=in_specs, out_specs=out_specs, check_vma=False)
```

time: 94.1 us -> 78 us (0.83)
  Pallas kernels: 92.2 us -> 76.8 us
    pallas_call x1, Pallas kernels: 92.2 us -> 76.8 us  [fused_shards(): pl.pallas_call(functools.partial(sublayer_kernel, rows_n, dp_n), out_shap...]
where the time goes in v2:
time: 78 us; the launch traced here: 77.8 us
  Pallas kernels  76.8 us (98%)
  local copies, waits for them, and re-layouts  1.02 us (1%)
    pallas_call x1, Pallas kernels, fused_shards(): pl.pallas_call(functools.partial(sublayer_kernel, rows_n, dp_n), out_shap...  76.8 us

profile of v2, /device:TPU:0, one launch (start us, length us, event | category | flops | bytes accessed | tf_op | source)
XLA Modules:
  0.0 77.8 jit_solution(9663753092445388457)
XLA Ops:
  0.0 76.8 %shard_map.46 = bf16[384,1536]{1,0:T(8,128)(2,1)S(1)} custom-call(bf16[384,1536]{1,0:T(8,128)(2,1)} %tok_hbm.1, f32[12,128]{1,0:T(8,128)} %bitcast.3, bf16[3,1536,1536]{2,1,0:T(8,128)(2,1)} %bitcast.2, bf16[1536,1536]{1,0:T(8,128)(2,1)} %wo_hbm.1), custom_call_target="tpu_custom_call" | custom-call | tf_op jit(solution)/shard_map/pallas_call | solution.py:550
  76.8 1.0 %copy.6 = bf16[384,1536]{1,0:T(8,128)(2,1)} copy(bf16[384,1536]{1,0:T(8,128)(2,1)S(1)} %shard_map.46) | data formatting | bytes 2359296

commit v3 on v2

--- a/solution.py
+++ b/solution.py
@@ -64,12 +64,29 @@
 ROWS = 32
 EXTRA = 16
 PIECE = 96
-SPAN = 1
 SKEW = 3
-LEAD = 2
-RETURN = 6
+LEAD = 1
 HAND = 12
 HAND_ON = 24
+
+
+def stream_starts(pairs, pieces, lag):
+    place, unit, starts, asked = 0, 0, [], {}
+    while unit < 3 * pairs * pieces:
+        following = len(starts)
+        if following < pairs - 2 and place >= asked.get(following, place + 1) + lag:
+            starts.append(place)
+            place += pieces
+            continue
+        if unit % (3 * pieces) == 2 * pieces:
+            asked[unit // (3 * pieces)] = place
+        unit += 1
+        place += 1
+    for pair in range(len(starts), pairs):
+        place = max(place, asked[pair] + lag)
+        starts.append(place)
+        place += pieces
+    return starts
 
 
 def sublayer_kernel(
@@ -89,8 +106,6 @@
     chunks = 3 * pairs
     pieces = tokens_n // PIECE
     units = chunks * pieces
-    span = SPAN * PIECE
-    spans = tokens_n // span
     tiles = block // WIDE
     quarter = WIDE // dp_n
     partner = {"col": 1 - col}
@@ -217,7 +232,7 @@
         )
 
     def attended_part(owner, d, p, i):
-        rows = pl.ds(pl.multiple_of(i * span, span), span)
+        rows = pl.ds(pl.multiple_of(i * PIECE, PIECE), PIECE)
         return attended.at[p, rows, head_columns(owner, d)]
 
     def attended_copy(d, p, i):
@@ -244,7 +259,7 @@
         )
 
     def attend_piece(d, p, i):
-        rows = pl.ds(pl.multiple_of(i * span, span), span)
+        rows = pl.ds(pl.multiple_of(i * PIECE, PIECE), PIECE)
         first = (col * 2 + d) * WIDE
         for h in range(2):
             at = slice(h * K, (h + 1) * K)
@@ -285,7 +300,7 @@
     def pair_ready(p):
         weights_ready(p)
         for d in range(2):
-            for i in range(spans):
+            for i in range(pieces):
                 cross_copy(d, p, i, 1 - col).wait_recv()
 
     def fold(p, rows, at):
@@ -353,7 +368,8 @@
         return jnp.where(pos > 0, LEAD + SKEW * pos, -pieces)
 
     end_offset = LEAD + SKEW * last_place
-    slots = units + end_offset + RETURN + SKEW * last_place
+    begins = stream_starts(pairs, pieces, end_offset + pieces + 1)
+    slots = begins[-1] + pieces + end_offset
     every = pl.ds(0, tokens_n)
 
     def fold_pair(p):
@@ -383,10 +399,19 @@
         for k in range(2):
             d = nearer if k == 0 else 1 - nearer
             pos = place(d)
-            u = t - offset(pos)
+            n = t - offset(pos)
+            u = n
+            returns = False
+            back_pair, back_piece = 0, 0
+            for p, begin in enumerate(begins):
+                inside = (n >= begin) & (n < begin + pieces)
+                returns = returns | inside
+                back_pair = jnp.where(inside, p, back_pair)
+                back_piece = jnp.where(inside, n - begin, back_piece)
+                u = jnp.where(n >= begin + pieces, u - pieces, u)
             c, i = u // pieces, u % pieces
 
-            @pl.when((u >= 0) & (u < units))
+            @pl.when((u >= 0) & (u < units) & jnp.logical_not(returns))
             def _():
                 rows = pl.ds(pl.multiple_of(i * PIECE, PIECE), PIECE)
 
@@ -435,41 +460,32 @@
                             whole = whole + spread_col[source, rows] * gain_all[source, c, :, lanes]
                         summed[d, c, rows, lanes] = whole.astype(bf16)
 
-                @pl.when((pos == last_place) & (c % 3 == 2) & (i % SPAN == SPAN - 1))
-                def _():
-                    p, s = c // 3, i // SPAN
-                    attend_piece(d, p, s)
-
-                    @pl.when(u < units - 1)
-                    def _():
-                        attended_copy(d, p, s).start()
-
-                    @pl.when(u == units - 1)
-                    def _():
-                        for o in range(last_place, 0, -1):
-                            direct_copy(d, p, s, o).start()
-
-                    cross_copy(d, p, s, col).start()
-
-        for k in range(2):
-            d = 1 - nearer if k == 0 else nearer
-            pos = place(d)
-            u = t - end_offset - RETURN - SKEW * (last_place - pos)
-            c, i = u // pieces, u % pieces
-            p = c // 3
-
-            @pl.when(
-                (pos < last_place) & (u >= 0) & (u < units) & (c % 3 == 2) & (i % SPAN == SPAN - 1)
-            )
+                @pl.when((pos == last_place) & (c % 3 == 2))
+                def _():
+                    attend_piece(d, c // 3, i)
+                    cross_copy(d, c // 3, i, col).start()
+
+            @pl.when(returns)
             def _():
-                s = i // SPAN
-                attended_copy(d, p, s).wait_recv()
-
-                @pl.when((pos > 0) & (u < units - 1))
-                def _():
-                    attended_copy(d, p, s).start()
-
-                cross_copy(d, p, s, col).start()
+                p, s, other = back_pair, back_piece, 1 - d
+                direct = (p == pairs - 1) & (s == pieces - 1)
+
+                @pl.when(pos > 0)
+                def _():
+                    attended_copy(other, p, s).wait_recv()
+
+                @pl.when((pos < last_place) & jnp.logical_not(direct))
+                def _():
+                    attended_copy(other, p, s).start()
+
+                @pl.when((pos == 0) & direct)
+                def _():
+                    for o in range(last_place, 0, -1):
+                        direct_copy(other, p, s, o).start()
+
+                @pl.when(pos > 0)
+                def _():
+                    cross_copy(other, p, s, col).start()
 
         @pl.when((t >= HAND) & (t < HAND + pieces * len(blocks)) & ((t - HAND) % pieces == 0))
         def _():
@@ -488,7 +504,7 @@
             across_copy(d, p, across_at).wait_recv()
             far_copy(d, p, across_at).start()
 
-        @pl.when(t == units + end_offset)
+        @pl.when(t == begins[pairs - 2] + pieces + end_offset)
         def _():
             for p in range(pairs - 2):
                 fold_pair(p)
@@ -497,8 +513,8 @@
     fold_pair(final - 1)
     weights_ready(final)
 
-    for i in range(spans):
-        rows = pl.ds(i * span, span)
+    for i in range(pieces):
+        rows = pl.ds(i * PIECE, PIECE)
         for d in range(2):
             cross_copy(d, final, i, 1 - col).wait_recv()
         for j in range(tiles // 2):
@@ -525,12 +541,12 @@
 
         @pl.when(pos > 0)
         def _():
-            sent(wide_w.at[0, 0, pl.ds(0, pairs * tokens_n - span)], at_send.at[d])
+            sent(wide_w.at[0, 0, pl.ds(0, pairs * tokens_n - PIECE)], at_send.at[d])
 
         @pl.when(pos == last_place)
         def _():
             for o in range(1, rows_n):
-                direct_copy(d, final, spans - 1, o).wait_send()
+                direct_copy(d, final, pieces - 1, o).wait_send()
 
     sent(summed.at[0, pl.ds(0, 2 * pairs)], la_send)
     for sem in (lx_send, ly_send, lc_send, ld_send):
@@ -541,7 +557,7 @@
     tokens_n, block = tokens.shape
     pairs = qkv_weight.shape[2] // (2 * WIDE)
     chunks = 3 * pairs
-    pieces, spans = tokens_n // PIECE, tokens_n // (SPAN * PIECE)
+    pieces = tokens_n // PIECE
     any_space = pl.BlockSpec(memory_space=pl.ANY)
     vmem = pl.BlockSpec(memory_space=pltpu.VMEM)
     hbm = pl.BlockSpec(memory_space=pltpu.HBM)
@@ -572,8 +588,8 @@
             dma((pieces,)), dma, dma((2, chunks)), dma((2, pairs)),
             dma((2,)), dma((rows_n,)), dma((2,)), dma((rows_n, chunks)),
             dma((2,)), dma((2, chunks, pieces)),
-            dma((2,)), dma((2, pairs, spans)), dma((rows_n,)),
-            dma, dma((2, pairs, spans)),
+            dma((2,)), dma((2, pairs, pieces)), dma((rows_n,)),
+            dma, dma((2, pairs, pieces)),
             dma, dma((2, pairs)), dma, dma((2, pairs)),
             dma, dma((2, pairs)), dma, dma((2, pairs)),
         ],
@@ -596,7 +612,7 @@
         fits = (
             cols_n == 2 and dp_n == 4 and rows_n >= 2 and qkv_weight.shape[2] % (2 * WIDE) == 0
             and qkv_weight.shape[2] >= 4 * WIDE
-            and block % (2 * WIDE) == 0 and tokens_n % (SPAN * PIECE) == 0
+            and block % (2 * WIDE) == 0 and tokens_n % PIECE == 0
             and (qkv_weight.shape[2] // (2 * WIDE)) * tokens_n <= block
         )
         if fits:

time: 78 us -> 75.7 us (0.971)
  Pallas kernels: 76.8 us -> 74.5 us
    pallas_call x1, Pallas kernels: 76.8 us -> 74.5 us  [fused_shards(): pl.pallas_call(functools.partial(sublayer_kernel, rows_n, dp_n), out_shap...]
where the time goes in v3:
time: 75.7 us; the launch traced here: 75.5 us
  Pallas kernels  74.5 us (98%)
  local copies, waits for them, and re-layouts  1.02 us (1%)
    pallas_call x1, Pallas kernels, fused_shards(): pl.pallas_call(functools.partial(sublayer_kernel, rows_n, dp_n), out_shap...  74.5 us

profile of v3, /device:TPU:0, one launch (start us, length us, event | category | flops | bytes accessed | tf_op | source)
XLA Modules:
  0.0 75.5 jit_solution(17806350777612272732)
XLA Ops:
  0.0 74.5 %shard_map.46 = bf16[384,1536]{1,0:T(8,128)(2,1)S(1)} custom-call(bf16[384,1536]{1,0:T(8,128)(2,1)} %tok_hbm.1, f32[12,128]{1,0:T(8,128)} %bitcast.3, bf16[3,1536,1536]{2,1,0:T(8,128)(2,1)} %bitcast.2, bf16[1536,1536]{1,0:T(8,128)(2,1)} %wo_hbm.1), custom_call_target="tpu_custom_call" | custom-call | tf_op jit(solution)/shard_map/pallas_call | solution.py:566
  74.5 1.0 %copy.6 = bf16[384,1536]{1,0:T(8,128)(2,1)} copy(bf16[384,1536]{1,0:T(8,128)(2,1)S(1)} %shard_map.46) | data formatting | bytes 2359296

commit v4 on v3

--- a/solution.py
+++ b/solution.py
@@ -64,10 +64,12 @@
 ROWS = 32
 EXTRA = 16
 PIECE = 96
+GROUP = 2
+DIRECT = 1
 SKEW = 3
 LEAD = 1
-HAND = 12
-HAND_ON = 24
+HAND = 16
+HAND_ON = 28
 
 
 def stream_starts(pairs, pieces, lag):
@@ -94,7 +96,7 @@
     tok, wide_w, gain_ref, gain_row, stat_col, stats, spread_col, normed, part, gain_sum, gain_all,
     arrived, summed, attended, late_w, total,
     tok_sem, gain_sem, w_sem, late_sem, st_send, st_recv, gs_send, gs_recv, rs_send, rs_recv,
-    at_send, at_recv, di_send, la_send, la_recv, lx_send, lx_recv, ly_send, ly_recv, lc_send, lc_recv,
+    at_send, at_recv, di_send, lp_recv, la_send, la_recv, lx_send, lx_recv, ly_send, ly_recv, lc_send, lc_recv,
     ld_send, ld_recv,
 ):
     z = lax.axis_index("row")
@@ -145,7 +147,7 @@
     def own_copy(d, p):
         rows = pl.ds(d * half + p * WIDE, WIDE)
         return pltpu.make_async_copy(
-            wo_hbm.at[rows], late_w.at[p, head_columns(col, d)], late_sem.at[d, p]
+            wo_hbm.at[rows], late_w.at[p, head_columns(col, d)], late_sem.at[p]
         )
 
     def quarter_at(owner, d, which):
@@ -157,14 +159,14 @@
         return pltpu.make_async_remote_copy(
             src_ref=wo_hbm.at[pl.ds(first, quarter)],
             dst_ref=late_w.at[p, quarter_at(owner, d, dp)],
-            send_sem=lx_send, recv_sem=lx_recv.at[d, p], device_id=partner,
+            send_sem=lx_send, recv_sem=lx_recv.at[p], device_id=partner,
             device_id_type=MESH,
         )
 
     def pass_copy(d, p, which, sends, recvs, device):
         piece = late_w.at[p, quarter_at(1 - col, d, which)]
         return pltpu.make_async_remote_copy(
-            src_ref=piece, dst_ref=piece, send_sem=sends, recv_sem=recvs.at[d, p],
+            src_ref=piece, dst_ref=piece, send_sem=sends, recv_sem=recvs.at[p],
             device_id=device, device_id_type=MESH,
         )
 
@@ -177,9 +179,22 @@
     def far_copy(d, p, which):
         return pass_copy(d, p, which, ld_send, ld_recv, sibling)
 
-    blocks = [(d, p) for p in range(pairs) for d in range(2)]
-    for d, p in blocks:
-        own_copy(d, p).start()
+    def whole(source, sem):
+        return pltpu.make_async_remote_copy(
+            src_ref=source, dst_ref=source, send_sem=sem, recv_sem=sem,
+            device_id=partner, device_id_type=MESH,
+        )
+
+    def sent(source, sem):
+        whole(source, sem).wait_send()
+
+    def landed(target, sem):
+        whole(target, sem).wait_recv()
+
+    @pl.loop(0, pairs)
+    def _(p):
+        own_copy(0, p).start()
+        own_copy(1, p).start()
 
     barrier = pltpu.get_barrier_semaphore()
     for o in range(1, rows_n):
@@ -219,8 +234,8 @@
 
     def gain_copy(d, c, source):
         return pltpu.make_async_remote_copy(
-            src_ref=gain_sum.at[d, c], dst_ref=gain_all.at[source, c], send_sem=gs_send.at[d],
-            recv_sem=gs_recv.at[source, c], device_id={"row": end_of(d)}, device_id_type=MESH,
+            src_ref=gain_sum.at[d, c], dst_ref=gain_all.at[c, source], send_sem=gs_send.at[d],
+            recv_sem=gs_recv.at[c], device_id={"row": end_of(d)}, device_id_type=MESH,
         )
 
     def sum_copy(d, c, i):
@@ -245,18 +260,27 @@
     def direct_copy(d, p, i, o):
         piece = attended_part(col, d, p, i)
         return pltpu.make_async_remote_copy(
-            src_ref=piece, dst_ref=piece, send_sem=di_send.at[o],
+            src_ref=piece, dst_ref=piece, send_sem=di_send,
             recv_sem=at_recv.at[d, p, i],
             device_id={"row": jnp.clip(jnp.where(d == 1, z - o, z + o), 0, last_place)},
             device_id_type=MESH,
         )
 
-    def cross_copy(d, p, i, owner):
+    def cross_copy(d, p, i, owner, recv_sem):
         piece = attended_part(owner, d, p, i)
         return pltpu.make_async_remote_copy(
             src_ref=piece, dst_ref=piece, send_sem=la_send,
-            recv_sem=la_recv.at[d, p, i], device_id=partner, device_id_type=MESH,
-        )
+            recv_sem=recv_sem, device_id=partner, device_id_type=MESH,
+        )
+
+    def cross_over(d, p, i):
+        @pl.when(p < pairs - 1)
+        def _():
+            cross_copy(d, p, i, col, lp_recv.at[jnp.minimum(p, pairs - 2)]).start()
+
+        @pl.when(p == pairs - 1)
+        def _():
+            cross_copy(d, p, i, col, la_recv.at[d, i]).start()
 
     def attend_piece(d, p, i):
         rows = pl.ds(pl.multiple_of(i * PIECE, PIECE), PIECE)
@@ -292,16 +316,14 @@
         spread_col[rows_n] = jnp.broadcast_to(scale, (128, tokens_n)).T
 
     def weights_ready(p):
-        for d in range(2):
-            own_copy(d, p).wait()
-            near_copy(d, p, sibling_at).wait_recv()
-            far_copy(d, p, (sibling_at + 2) % dp_n).wait_recv()
+        rows = late_w.at[p, pl.ds(0, 2 * WIDE)]
+        pltpu.make_async_copy(rows, rows, late_sem.at[p]).wait()
+        for recvs in (lc_recv, ld_recv):
+            landed(late_w.at[p, pl.ds(0, 2 * quarter)], recvs.at[p])
 
     def pair_ready(p):
         weights_ready(p)
-        for d in range(2):
-            for i in range(pieces):
-                cross_copy(d, p, i, 1 - col).wait_recv()
+        landed(summed.at[0, pl.ds(0, 2)], lp_recv.at[p])
 
     def fold(p, rows, at):
         return jnp.dot(attended[p, rows, :], late_w[p, :, at], preferred_element_type=f32)
@@ -429,9 +451,8 @@
 
                     @pl.when(pos == last_place)
                     def _():
-                        gain_all[z, c] = gain_value
-                        for o in range(1, rows_n):
-                            gain_copy(d, c, lax.rem(z + o, rows_n)).wait_recv()
+                        gain_all[c, z] = gain_value
+                        landed(gain_all.at[c, pl.ds(0, last_place)], gs_recv.at[c])
 
                 @pl.when(pos == 0)
                 def _():
@@ -457,18 +478,20 @@
                         whole = part[d, rows, lanes] + arrived[d, c, rows, lanes].astype(f32)
                         whole = whole * scale
                         for source in range(rows_n):
-                            whole = whole + spread_col[source, rows] * gain_all[source, c, :, lanes]
+                            whole = whole + spread_col[source, rows] * gain_all[c, source, :, lanes]
                         summed[d, c, rows, lanes] = whole.astype(bf16)
 
                 @pl.when((pos == last_place) & (c % 3 == 2))
                 def _():
                     attend_piece(d, c // 3, i)
-                    cross_copy(d, c // 3, i, col).start()
+                    cross_over(d, c // 3, i)
 
             @pl.when(returns)
             def _():
-                p, s, other = back_pair, back_piece, 1 - d
-                direct = (p == pairs - 1) & (s == pieces - 1)
+                p, other = back_pair, 1 - d
+                turned = (p == pairs - 1) & (pos == last_place)
+                s = jnp.where(turned, (back_piece + pieces - DIRECT) % pieces, back_piece)
+                direct = (p == pairs - 1) & (s >= pieces - DIRECT)
 
                 @pl.when(pos > 0)
                 def _():
@@ -485,24 +508,25 @@
 
                 @pl.when(pos > 0)
                 def _():
-                    cross_copy(other, p, s, col).start()
-
-        @pl.when((t >= HAND) & (t < HAND + pieces * len(blocks)) & ((t - HAND) % pieces == 0))
-        def _():
-            b = (t - HAND) // pieces
-            d, p = b % 2, b // 2
-            share_copy(d, p, 1 - col).wait_recv()
-            across_copy(d, p, dp).start()
-            near_copy(d, p, dp).start()
+                    cross_over(other, p, s)
+
+        @pl.when((t >= HAND) & (t < HAND + 2 * pieces * pairs) & ((t - HAND) % (2 * pieces) == 0))
+        def _():
+            p = (t - HAND) // (2 * pieces)
+            landed(late_w.at[p, pl.ds(0, 2 * quarter)], lx_recv.at[p])
+            for d in range(2):
+                across_copy(d, p, dp).start()
+                near_copy(d, p, dp).start()
 
         @pl.when(
-            (t >= HAND_ON) & (t < HAND_ON + pieces * len(blocks)) & ((t - HAND_ON) % pieces == 0)
-        )
-        def _():
-            b = (t - HAND_ON) // pieces
-            d, p = b % 2, b // 2
-            across_copy(d, p, across_at).wait_recv()
-            far_copy(d, p, across_at).start()
+            (t >= HAND_ON) & (t < HAND_ON + 2 * pieces * pairs)
+            & ((t - HAND_ON) % (2 * pieces) == 0)
+        )
+        def _():
+            p = (t - HAND_ON) // (2 * pieces)
+            landed(late_w.at[p, pl.ds(0, 2 * quarter)], ly_recv.at[p])
+            for d in range(2):
+                far_copy(d, p, across_at).start()
 
         @pl.when(t == begins[pairs - 2] + pieces + end_offset)
         def _():
@@ -513,19 +537,25 @@
     fold_pair(final - 1)
     weights_ready(final)
 
-    for i in range(pieces):
-        rows = pl.ds(i * PIECE, PIECE)
+    def fold_owner(rows, at, owner):
+        heads = pl.ds(pl.multiple_of(owner * 2 * WIDE, 2 * WIDE), 2 * WIDE)
+        return jnp.dot(
+            attended[final, rows, heads], late_w[final, heads, at], preferred_element_type=f32
+        )
+
+    for j in range(tiles // 2):
+        at = slice(j * 2 * WIDE, (j + 1) * 2 * WIDE)
+        total[:, at] = total[:, at] + fold_owner(every, at, col)
+
+    for first in range(0, pieces, GROUP):
+        group = range(first, min(first + GROUP, pieces))
+        rows = slice(first * PIECE, (group[-1] + 1) * PIECE)
         for d in range(2):
-            cross_copy(d, final, i, 1 - col).wait_recv()
+            for i in group:
+                cross_copy(d, final, i, 1 - col, la_recv.at[d, i]).wait_recv()
         for j in range(tiles // 2):
             at = slice(j * 2 * WIDE, (j + 1) * 2 * WIDE)
-            out[rows, at] = (total[rows, at] + fold(final, rows, at)).astype(bf16)
-
-    def sent(source, sem):
-        pltpu.make_async_remote_copy(
-            src_ref=source, dst_ref=source, send_sem=sem, recv_sem=lx_recv.at[0, 0],
-            device_id=partner, device_id_type=MESH,
-        ).wait_send()
+            out[rows, at] = (total[rows, at] + fold_owner(rows, at, 1 - col)).astype(bf16)
 
     for which in range(2):
         @pl.when(z != which * last_place)
@@ -541,12 +571,11 @@
 
         @pl.when(pos > 0)
         def _():
-            sent(wide_w.at[0, 0, pl.ds(0, pairs * tokens_n - PIECE)], at_send.at[d])
+            sent(wide_w.at[0, 0, pl.ds(0, pairs * tokens_n - DIRECT * PIECE)], at_send.at[d])
 
         @pl.when(pos == last_place)
         def _():
-            for o in range(1, rows_n):
-                direct_copy(d, final, pieces - 1, o).wait_send()
+            sent(wide_w.at[0, 0, pl.ds(0, last_place * DIRECT * PIECE)], di_send)
 
     sent(summed.at[0, pl.ds(0, 2 * pairs)], la_send)
     for sem in (lx_send, ly_send, lc_send, ld_send):
@@ -579,19 +608,18 @@
             pltpu.VMEM((tokens_n + EXTRA, block), bf16),
             pltpu.VMEM((2, tokens_n, WIDE), f32),
             pltpu.VMEM((2, chunks, 1, WIDE), f32),
-            pltpu.VMEM((rows_n, chunks, 1, WIDE), f32),
+            pltpu.VMEM((chunks, rows_n, 1, WIDE), f32),
             pltpu.VMEM((2, chunks, tokens_n, WIDE), bf16),
             pltpu.VMEM((2, chunks, tokens_n, WIDE), bf16),
             pltpu.VMEM((pairs, tokens_n, 4 * WIDE), bf16),
             pltpu.VMEM((pairs, 4 * WIDE, block), bf16),
             pltpu.VMEM((tokens_n, block), f32),
-            dma((pieces,)), dma, dma((2, chunks)), dma((2, pairs)),
-            dma((2,)), dma((rows_n,)), dma((2,)), dma((rows_n, chunks)),
+            dma((pieces,)), dma, dma((2, chunks)), dma((pairs,)),
+            dma((2,)), dma((rows_n,)), dma((2,)), dma((chunks,)),
             dma((2,)), dma((2, chunks, pieces)),
-            dma((2,)), dma((2, pairs, pieces)), dma((rows_n,)),
-            dma, dma((2, pairs, pieces)),
-            dma, dma((2, pairs)), dma, dma((2, pairs)),
-            dma, dma((2, pairs)), dma, dma((2, pairs)),
+            dma((2,)), dma((2, pairs, pieces)), dma, dma((pairs - 1,)),
+            dma, dma((2, pieces)), dma, dma((pairs,)), dma, dma((pairs,)),
+            dma, dma((pairs,)), dma, dma((pairs,)),
         ],
         compiler_params=pltpu.CompilerParams(
             collective_id=0, has_side_effects=True, vmem_limit_bytes=65800000
@@ -614,6 +642,7 @@
             and qkv_weight.shape[2] >= 4 * WIDE
             and block % (2 * WIDE) == 0 and tokens_n % PIECE == 0
             and (qkv_weight.shape[2] // (2 * WIDE)) * tokens_n <= block
+            and (rows_n - 1) * DIRECT * PIECE <= block and tokens_n > DIRECT * PIECE
         )
         if fits:
             return fused_shards(rows_n, dp_n, tokens, norm_gain, qkv_weight, out_weight)

time: 75.7 us -> 74.1 us (0.979)
  Pallas kernels: 74.5 us -> 72.9 us
    pallas_call x1, Pallas kernels: 74.5 us -> 72.9 us  [fused_shards(): pl.pallas_call(functools.partial(sublayer_kernel, rows_n, dp_n), out_shap...]
where the time goes in v4:
time: 74.1 us; the launch traced here: 73.9 us
  Pallas kernels  72.9 us (98%)
  local copies, waits for them, and re-layouts  1.02 us (1%)
    pallas_call x1, Pallas kernels, fused_shards(): pl.pallas_call(functools.partial(sublayer_kernel, rows_n, dp_n), out_shap...  72.9 us

profile of v4, /device:TPU:0, one launch (start us, length us, event | category | flops | bytes accessed | tf_op | source)
XLA Modules:
  0.0 73.9 jit_solution(17171037465693637583)
XLA Ops:
  0.0 72.9 %shard_map.46 = bf16[384,1536]{1,0:T(8,128)(2,1)S(1)} custom-call(bf16[384,1536]{1,0:T(8,128)(2,1)} %tok_hbm.1, f32[12,128]{1,0:T(8,128)} %bitcast.3, bf16[3,1536,1536]{2,1,0:T(8,128)(2,1)} %bitcast.2, bf16[1536,1536]{1,0:T(8,128)(2,1)} %wo_hbm.1), custom_call_target="tpu_custom_call" | custom-call | tf_op jit(solution)/shard_map/pallas_call | solution.py:595
  72.9 1.0 %copy.6 = bf16[384,1536]{1,0:T(8,128)(2,1)} copy(bf16[384,1536]{1,0:T(8,128)(2,1)S(1)} %shard_map.46) | data formatting | bytes 2359296

commit v5 on v4

--- a/solution.py
+++ b/solution.py
@@ -66,29 +66,34 @@
 PIECE = 96
 GROUP = 2
 DIRECT = 1
+EARLY = 3
 SKEW = 3
 LEAD = 1
 HAND = 16
 HAND_ON = 28
 
 
-def stream_starts(pairs, pieces, lag):
-    place, unit, starts, asked = 0, 0, [], {}
+def stream_blocks(pairs, pieces, lag):
+    place, unit, blocks, asked = 0, 0, [], {}
+    early = min(EARLY, pieces)
     while unit < 3 * pairs * pieces:
-        following = len(starts)
-        if following < pairs - 2 and place >= asked.get(following, place + 1) + lag:
-            starts.append(place)
-            place += pieces
+        following = len(blocks)
+        if early and following < pairs - 2 and place >= asked.get(following, place + 1) + lag:
+            blocks.append((following, 0, early, place))
+            place += early
             continue
         if unit % (3 * pieces) == 2 * pieces:
             asked[unit // (3 * pieces)] = place
         unit += 1
         place += 1
-    for pair in range(len(starts), pairs):
-        place = max(place, asked[pair] + lag)
-        starts.append(place)
-        place += pieces
-    return starts
+    gone = len(blocks)
+    for pair in range(pairs):
+        first = early if pair < gone else 0
+        if first < pieces:
+            place = max(place, asked[pair] + first + lag)
+            blocks.append((pair, first, pieces - first, place))
+            place += pieces - first
+    return blocks
 
 
 def sublayer_kernel(
@@ -364,10 +369,6 @@
     def _():
         sum_copy(nearer, 0, 0).start()
 
-    @pl.loop(0, pairs)
-    def _(p):
-        share_copy(0, p, col).start()
-        share_copy(1, p, col).start()
 
     @pl.loop(1, pieces)
     def _(i):
@@ -390,8 +391,8 @@
         return jnp.where(pos > 0, LEAD + SKEW * pos, -pieces)
 
     end_offset = LEAD + SKEW * last_place
-    begins = stream_starts(pairs, pieces, end_offset + pieces + 1)
-    slots = begins[-1] + pieces + end_offset
+    blocks = stream_blocks(pairs, pieces, end_offset + pieces + 1)
+    slots = blocks[-1][3] + pieces + end_offset
     every = pl.ds(0, tokens_n)
 
     def fold_pair(p):
@@ -403,8 +404,34 @@
 
     stat_slot = jnp.where(starts, 0, LEAD + SKEW + 1)
 
+    def multiply(d, c, pos):
+        weight_copy(d, c).wait()
+        value = jnp.dot(normed[...], wide_w[d, c], preferred_element_type=f32)
+        part[d, c % 2] = value[0:tokens_n]
+        gain_value = value[tokens_n:tokens_n + 1] + value[tokens_n + 1:tokens_n + 2]
+
+        @pl.when(pos < last_place)
+        def _():
+            gain_sum[d, c] = gain_value
+            gain_copy(d, c, z).start()
+
+        @pl.when(pos == last_place)
+        def _():
+            gain_all[c, z] = gain_value
+
+    @pl.when(starts)
+    def _():
+        multiply(nearer, 1, 0)
+
     @pl.loop(0, slots)
     def _(t):
+        @pl.when(t == stat_slot + 1)
+        def _():
+            @pl.loop(0, pairs)
+            def _(p):
+                share_copy(0, p, col).start()
+                share_copy(1, p, col).start()
+
         @pl.when(t == stat_slot)
         def _():
             stats[z, 0] = stat_col[0].T[0:1]
@@ -418,6 +445,7 @@
         def _():
             spread_statistics()
 
+        ahead = []
         for k in range(2):
             d = nearer if k == 0 else 1 - nearer
             pos = place(d)
@@ -425,38 +453,27 @@
             u = n
             returns = False
             back_pair, back_piece = 0, 0
-            for p, begin in enumerate(begins):
-                inside = (n >= begin) & (n < begin + pieces)
+            for p, piece, count, begin in blocks:
+                inside = (n >= begin) & (n < begin + count)
                 returns = returns | inside
                 back_pair = jnp.where(inside, p, back_pair)
-                back_piece = jnp.where(inside, n - begin, back_piece)
-                u = jnp.where(n >= begin + pieces, u - pieces, u)
+                back_piece = jnp.where(inside, n - begin + piece, back_piece)
+                u = jnp.where(n >= begin + count, u - count, u)
             c, i = u // pieces, u % pieces
 
             @pl.when((u >= 0) & (u < units) & jnp.logical_not(returns))
             def _():
                 rows = pl.ds(pl.multiple_of(i * PIECE, PIECE), PIECE)
 
-                @pl.when(i == 0)
-                def _():
-                    weight_copy(d, c).wait()
-                    value = jnp.dot(normed[...], wide_w[d, c], preferred_element_type=f32)
-                    part[d] = value[0:tokens_n]
-                    gain_value = value[tokens_n:tokens_n + 1] + value[tokens_n + 1:tokens_n + 2]
-
-                    @pl.when(pos < last_place)
-                    def _():
-                        gain_sum[d, c] = gain_value
-                        gain_copy(d, c, z).start()
-
-                    @pl.when(pos == last_place)
-                    def _():
-                        gain_all[c, z] = gain_value
-                        landed(gain_all.at[c, pl.ds(0, last_place)], gs_recv.at[c])
+                side = c % 2
+
+                @pl.when((i == 0) & (pos == last_place))
+                def _():
+                    landed(gain_all.at[c, pl.ds(0, last_place)], gs_recv.at[c])
 
                 @pl.when(pos == 0)
                 def _():
-                    summed[d, c, rows] = part[d, rows].astype(bf16)
+                    summed[d, c, rows] = part[d, side, rows].astype(bf16)
 
                 @pl.when(pos > 0)
                 def _():
@@ -464,7 +481,7 @@
 
                 @pl.when((pos > 0) & (pos < last_place))
                 def _():
-                    summed[d, c, rows] = (part[d, rows] + arrived[d, c, rows].astype(f32)).astype(bf16)
+                    summed[d, c, rows] = (part[d, side, rows] + arrived[d, c, rows].astype(f32)).astype(bf16)
 
                 @pl.when(pos < last_place)
                 def _():
@@ -475,7 +492,7 @@
                     scale = spread_col[rows_n, rows]
                     for h in range(2):
                         lanes = slice(h * 128, (h + 1) * 128)
-                        whole = part[d, rows, lanes] + arrived[d, c, rows, lanes].astype(f32)
+                        whole = part[d, side, rows, lanes] + arrived[d, c, rows, lanes].astype(f32)
                         whole = whole * scale
                         for source in range(rows_n):
                             whole = whole + spread_col[source, rows] * gain_all[c, source, :, lanes]
@@ -485,6 +502,10 @@
                 def _():
                     attend_piece(d, c // 3, i)
                     cross_over(d, c // 3, i)
+
+            ahead.append(
+                (d, pos, u + 1, (u >= -1) & (u < units - 1) & jnp.logical_not(returns))
+            )
 
             @pl.when(returns)
             def _():
@@ -510,6 +531,11 @@
                 def _():
                     cross_over(other, p, s)
 
+        for d, pos, u, due in ahead:
+            @pl.when(due & (u % pieces == 0))
+            def _():
+                multiply(d, u // pieces, pos)
+
         @pl.when((t >= HAND) & (t < HAND + 2 * pieces * pairs) & ((t - HAND) % (2 * pieces) == 0))
         def _():
             p = (t - HAND) // (2 * pieces)
@@ -528,7 +554,7 @@
             for d in range(2):
                 far_copy(d, p, across_at).start()
 
-        @pl.when(t == begins[pairs - 2] + pieces + end_offset)
+        @pl.when(t == blocks[-2][3] + blocks[-2][2] + end_offset)
         def _():
             for p in range(pairs - 2):
                 fold_pair(p)
@@ -606,7 +632,7 @@
             pltpu.VMEM((rows_n, 2, 1, tokens_n), f32),
             pltpu.VMEM((rows_n + 1, tokens_n, 128), f32),
             pltpu.VMEM((tokens_n + EXTRA, block), bf16),
-            pltpu.VMEM((2, tokens_n, WIDE), f32),
+            pltpu.VMEM((2, 2, tokens_n, WIDE), f32),
             pltpu.VMEM((2, chunks, 1, WIDE), f32),
             pltpu.VMEM((chunks, rows_n, 1, WIDE), f32),
             pltpu.VMEM((2, chunks, tokens_n, WIDE), bf16),

time: 74.1 us -> 73.1 us (0.987)
  Pallas kernels: 72.9 us -> 71.9 us
    pallas_call x1, Pallas kernels: 72.9 us -> 71.9 us  [fused_shards(): pl.pallas_call(functools.partial(sublayer_kernel, rows_n, dp_n), out_shap...]
where the time goes in v5:
time: 73.1 us; the launch traced here: 73 us
  Pallas kernels  71.9 us (98%)
  local copies, waits for them, and re-layouts  1.02 us (1%)
    pallas_call x1, Pallas kernels, fused_shards(): pl.pallas_call(functools.partial(sublayer_kernel, rows_n, dp_n), out_shap...  71.9 us

profile of v5, /device:TPU:0, one launch (start us, length us, event | category | flops | bytes accessed | tf_op | source)
XLA Modules:
  0.0 73.0 jit_solution(14224840831474520989)
XLA Ops:
  0.0 71.9 %shard_map.46 = bf16[384,1536]{1,0:T(8,128)(2,1)S(1)} custom-call(bf16[384,1536]{1,0:T(8,128)(2,1)} %tok_hbm.1, f32[12,128]{1,0:T(8,128)} %bitcast.3, bf16[3,1536,1536]{2,1,0:T(8,128)(2,1)} %bitcast.2, bf16[1536,1536]{1,0:T(8,128)(2,1)} %wo_hbm.1), custom_call_target="tpu_custom_call" | custom-call | tf_op jit(solution)/shard_map/pallas_call | solution.py:621
  71.9 1.0 %copy.6 = bf16[384,1536]{1,0:T(8,128)(2,1)} copy(bf16[384,1536]{1,0:T(8,128)(2,1)S(1)} %shard_map.46) | data formatting | bytes 2359296

commit v6 on v5

--- a/solution.py
+++ b/solution.py
@@ -69,8 +69,8 @@
 EARLY = 3
 SKEW = 3
 LEAD = 1
-HAND = 16
-HAND_ON = 28
+HAND = 18
+HAND_ON = 32
 
 
 def stream_blocks(pairs, pieces, lag):
@@ -101,7 +101,7 @@
     tok, wide_w, gain_ref, gain_row, stat_col, stats, spread_col, normed, part, gain_sum, gain_all,
     arrived, summed, attended, late_w, total,
     tok_sem, gain_sem, w_sem, late_sem, st_send, st_recv, gs_send, gs_recv, rs_send, rs_recv,
-    at_send, at_recv, di_send, lp_recv, la_send, la_recv, lx_send, lx_recv, ly_send, ly_recv, lc_send, lc_recv,
+    at_send, at_recv, ah_recv, di_send, lp_recv, la_send, la_recv, lx_send, lx_recv, ly_send, ly_recv, lc_send, lc_recv,
     ld_send, ld_recv,
 ):
     z = lax.axis_index("row")
@@ -141,7 +141,13 @@
     def _(i):
         tok_copy(i).start()
 
-    @pl.loop(0, chunks)
+    early_side = jnp.where(2 * z < rows_n - 1, 1, 0)
+    for c in range(2):
+        weight_copy(early_side, c).start()
+    for c in range(2):
+        weight_copy(1 - early_side, c).start()
+
+    @pl.loop(2, chunks)
     def _(c):
         weight_copy(0, c).start()
         weight_copy(1, c).start()
@@ -247,7 +253,7 @@
         at = pl.ds(pl.multiple_of(i * PIECE, PIECE), PIECE)
         return pltpu.make_async_remote_copy(
             src_ref=summed.at[d, c, at], dst_ref=arrived.at[d, c, at],
-            send_sem=rs_send.at[d], recv_sem=rs_recv.at[d, c, i],
+            send_sem=rs_send.at[d], recv_sem=rs_recv.at[d, (c * pieces + i) % rs_recv.shape[1]],
             device_id=onward(d), device_id_type=MESH,
         )
 
@@ -260,6 +266,24 @@
         return pltpu.make_async_remote_copy(
             src_ref=piece, dst_ref=piece, send_sem=at_send.at[d],
             recv_sem=at_recv.at[d, p, i], device_id=back(d), device_id_type=MESH,
+        )
+
+    def half_part(owner, d, i, h):
+        first = pl.multiple_of(i * PIECE + h * (PIECE // 2), PIECE // 2)
+        return attended.at[pairs - 1, pl.ds(first, PIECE // 2), head_columns(owner, d)]
+
+    def half_copy(d, i, h):
+        piece = half_part(col, d, i, h)
+        return pltpu.make_async_remote_copy(
+            src_ref=piece, dst_ref=piece, send_sem=at_send.at[d],
+            recv_sem=ah_recv.at[d, i, h], device_id=back(d), device_id_type=MESH,
+        )
+
+    def half_cross(d, i, h):
+        piece = half_part(col, d, i, h)
+        return pltpu.make_async_remote_copy(
+            src_ref=piece, dst_ref=piece, send_sem=la_send,
+            recv_sem=la_recv.at[d, i], device_id=partner, device_id_type=MESH,
         )
 
     def direct_copy(d, p, i, o):
@@ -425,7 +449,7 @@
 
     @pl.loop(0, slots)
     def _(t):
-        @pl.when(t == stat_slot + 1)
+        @pl.when(t == stat_slot + 4)
         def _():
             @pl.loop(0, pairs)
             def _(p):
@@ -514,11 +538,28 @@
                 s = jnp.where(turned, (back_piece + pieces - DIRECT) % pieces, back_piece)
                 direct = (p == pairs - 1) & (s >= pieces - DIRECT)
 
-                @pl.when(pos > 0)
+                halved = (p == pairs - 1) & jnp.logical_not(direct)
+
+                @pl.when(halved)
+                def _():
+                    for h in range(2):
+                        @pl.when(pos > 0)
+                        def _():
+                            half_copy(other, s, h).wait_recv()
+
+                        @pl.when(pos < last_place)
+                        def _():
+                            half_copy(other, s, h).start()
+
+                        @pl.when(pos > 0)
+                        def _():
+                            half_cross(other, s, h).start()
+
+                @pl.when(jnp.logical_not(halved) & (pos > 0))
                 def _():
                     attended_copy(other, p, s).wait_recv()
 
-                @pl.when((pos < last_place) & jnp.logical_not(direct))
+                @pl.when((pos < last_place) & jnp.logical_not(halved | direct))
                 def _():
                     attended_copy(other, p, s).start()
 
@@ -527,7 +568,7 @@
                     for o in range(last_place, 0, -1):
                         direct_copy(other, p, s, o).start()
 
-                @pl.when(pos > 0)
+                @pl.when(jnp.logical_not(halved) & (pos > 0))
                 def _():
                     cross_over(other, p, s)
 
@@ -642,8 +683,8 @@
             pltpu.VMEM((tokens_n, block), f32),
             dma((pieces,)), dma, dma((2, chunks)), dma((pairs,)),
             dma((2,)), dma((rows_n,)), dma((2,)), dma((chunks,)),
-            dma((2,)), dma((2, chunks, pieces)),
-            dma((2,)), dma((2, pairs, pieces)), dma, dma((pairs - 1,)),
+            dma((2,)), dma((2, min(chunks * pieces, 2 * (LEAD + SKEW * (rows_n - 1) + pieces)))),
+            dma((2,)), dma((2, pairs, pieces)), dma((2, pieces, 2)), dma, dma((pairs - 1,)),
             dma, dma((2, pieces)), dma, dma((pairs,)), dma, dma((pairs,)),
             dma, dma((pairs,)), dma, dma((pairs,)),
         ],

time: 73.1 us -> 72.6 us (level)
  no operation moved by 1% of the time
where the time goes in v6:
time: 72.6 us; the launch traced here: 72.4 us
  Pallas kernels  71.4 us (98%)
  local copies, waits for them, and re-layouts  1.02 us (1%)
    pallas_call x1, Pallas kernels, fused_shards(): pl.pallas_call(functools.partial(sublayer_kernel, rows_n, dp_n), out_shap...  71.4 us

profile of v6, /device:TPU:0, one launch (start us, length us, event | category | flops | bytes accessed | tf_op | source)
XLA Modules:
  0.0 72.4 jit_solution(15329822359015600537)
XLA Ops:
  0.0 71.4 %shard_map.46 = bf16[384,1536]{1,0:T(8,128)(2,1)S(1)} custom-call(bf16[384,1536]{1,0:T(8,128)(2,1)} %tok_hbm.1, f32[12,128]{1,0:T(8,128)} %bitcast.3, bf16[3,1536,1536]{2,1,0:T(8,128)(2,1)} %bitcast.2, bf16[1536,1536]{1,0:T(8,128)(2,1)} %wo_hbm.1), custom_call_target="tpu_custom_call" | custom-call | tf_op jit(solution)/shard_map/pallas_call | solution.py:662
  71.4 1.0 %copy.6 = bf16[384,1536]{1,0:T(8,128)(2,1)} copy(bf16[384,1536]{1,0:T(8,128)(2,1)S(1)} %shard_map.46) | data formatting | bytes 2359296

commit v7 on v6

--- a/solution.py
+++ b/solution.py
@@ -69,8 +69,8 @@
 EARLY = 3
 SKEW = 3
 LEAD = 1
-HAND = 18
-HAND_ON = 32
+HAND = 20
+HAND_ON = 34
 
 
 def stream_blocks(pairs, pieces, lag):

time: 72.6 us -> 72.7 us (level)
  no operation moved by 1% of the time
where the time goes in v7:
time: 72.7 us; the launch traced here: 72.5 us
  Pallas kernels  71.5 us (98%)
  local copies, waits for them, and re-layouts  1.02 us (1%)
    pallas_call x1, Pallas kernels, fused_shards(): pl.pallas_call(functools.partial(sublayer_kernel, rows_n, dp_n), out_shap...  71.5 us

profile of v7, /device:TPU:0, one launch (start us, length us, event | category | flops | bytes accessed | tf_op | source)
XLA Modules:
  0.0 72.5 jit_solution(10731509554141127331)
XLA Ops:
  0.0 71.5 %shard_map.46 = bf16[384,1536]{1,0:T(8,128)(2,1)S(1)} custom-call(bf16[384,1536]{1,0:T(8,128)(2,1)} %tok_hbm.1, f32[12,128]{1,0:T(8,128)} %bitcast.3, bf16[3,1536,1536]{2,1,0:T(8,128)(2,1)} %bitcast.2, bf16[1536,1536]{1,0:T(8,128)(2,1)} %wo_hbm.1), custom_call_target="tpu_custom_call" | custom-call | tf_op jit(solution)/shard_map/pallas_call | solution.py:662
  71.5 1.0 %copy.6 = bf16[384,1536]{1,0:T(8,128)(2,1)} copy(bf16[384,1536]{1,0:T(8,128)(2,1)S(1)} %shard_map.46) | data formatting | bytes 2359296
